TPU v7x, 32 devices: a whole 2x2x4 slice. The times are simulated.
32 devices in a mesh: seq: 16 (over z, y, x), head: 2 (over core).
Axes of the slice: x: 2, y: 2, z: 4, core: 2. Of those that a mesh axis runs over, the one named last changes fastest.
Arguments:
- hidden_state_input: bfloat16 [16, 8192], P(None, 'seq'), may hold values from -40 to 40
- attention_norm_gain: bfloat16 [8192], P('seq'), may hold values from 0.099609375 to 1.8984375
- query_projection_matrix: bfloat16 [8192, 8192], P('seq', 'head'), may hold values from -0.0625 to 0.0625
- key_projection_matrix: bfloat16 [8192, 1024], P('seq', 'head'), may hold values from -0.0625 to 0.0625
- value_projection_matrix: bfloat16 [8192, 1024], P('seq', 'head'), may hold values from -0.0625 to 0.0625
- output_projection_matrix: bfloat16 [8192, 8192], P('head', 'seq'), may hold values from -0.25 to 0.25
- adapter_down_matrix: bfloat16 [512, 16, 8192], P('head', None, 'seq'), may hold values from -0.0625 to 0.0625
- adapter_up_matrix: bfloat16 [512, 16, 8192], P('seq', None, 'head'), may hold values from -3 to 3
- adapter_choice_index: int32 [16], replicated, may hold values from 0 to 511
- lengths: int32 [16], replicated, may hold values from 4 to 4096
- rotated_key_cache: bfloat16 [16, 4096, 8, 128], P(None, 'seq', 'head'), may hold values from -200 to 200
- cached_value_rows: bfloat16 [16, 4096, 8, 128], P(None, 'seq', 'head'), may hold values from -24 to 24
Outputs:
- output_sum: bfloat16 [16, 8192], P(None, 'seq')
Inputs may be any that keep to these rules, and one draw needn't show every extreme that they name: `adapter_choice_index`: index of the adapter that serves each request. The new token stands at position lengths[r]; cache entries at lengths[r] and beyond are not read.
All inputs are finite; a program needn't handle non-finite values.
Results may differ from a plain program's by a relative error of at most 0.025.
Values may be sent and summed in bfloat16 or wider, within the bound.
No kernel may reach another device: no remote copies, remote signals or barrier semaphores. Data moves between devices by JAX's collectives and lax.ppermute only.
A program may use at most 64 MiB of HBM per device.

v0:
```python
import jax
import jax.numpy as jnp
from jax import lax
from jax.sharding import PartitionSpec as P

norm_epsilon = 1e-05
adapter_scale_factor = 1.0
rope_base = 500000.0
masked_score = -1e30


def joined(value, axis, combine):
    everything = jax.tree.map(
        lambda part, kind: lax.all_gather(part.astype(kind), axis),
        value,
        (jnp.bfloat16, jnp.bfloat16, jnp.bfloat16),
    )

    def take(k):
        return jax.tree.map(lambda part, own: part[k].astype(own.dtype), everything, value)

    return lax.fori_loop(
        1, lax.axis_size(axis), lambda k, so_far: combine(so_far, take(k)), take(0)
    )


def rotate(vectors, positions):
    half_dim = vectors.shape[-1] // 2
    frequency = jnp.exp(
        -jnp.arange(half_dim, dtype=jnp.float32) * (jnp.log(jnp.float32(rope_base)) / half_dim)
    )
    angles = positions.astype(jnp.float32)[:, None] * frequency[None, :]
    cosine = jnp.cos(angles)[:, None, :]
    sine_val = jnp.sin(angles)[:, None, :]
    lower_half = vectors[..., :half_dim]
    upper_half = vectors[..., half_dim:]
    return jnp.concatenate(
        [lower_half * cosine - upper_half * sine_val, upper_half * cosine + lower_half * sine_val],
        axis=-1,
    )


def combine_parts(earlier, later):
    max_one, sum_one, out_one = earlier
    max_two, sum_two, out_two = later
    overall = jnp.maximum(max_one, max_two)
    scale_one = jnp.exp(max_one - overall)
    scale_two = jnp.exp(max_two - overall)
    return (
        overall,
        sum_one * scale_one + sum_two * scale_two,
        out_one * scale_one[..., None] + out_two * scale_two[..., None],
    )


def body(
    hidden_state_input,
    attention_norm_gain,
    query_projection_matrix,
    key_projection_matrix,
    value_projection_matrix,
    output_projection_matrix,
    adapter_down_matrix,
    adapter_up_matrix,
    adapter_choice_index,
    lengths,
    rotated_key_cache,
    cached_value_rows,
):
    requests = hidden_state_input.shape[0]
    width_part = hidden_state_input.shape[1]
    cached = rotated_key_cache.shape[1]
    kv_local = rotated_key_cache.shape[2]
    head_dim = rotated_key_cache.shape[3]
    query_cols = query_projection_matrix.shape[1]
    heads_local = query_cols // head_dim
    group_size = heads_local // kv_local
    seq_index = lax.axis_index("seq")
    head_index = lax.axis_index("head")
    model_width = width_part * lax.axis_size("seq")
    values32 = hidden_state_input.astype(jnp.float32)
    square_part = jnp.sum(values32 * values32, axis=1)
    scaled = (values32 * attention_norm_gain.astype(jnp.float32)[None, :]).astype(jnp.bfloat16)
    query_part = jnp.dot(scaled, query_projection_matrix, preferred_element_type=jnp.float32)
    key_part = jnp.dot(scaled, key_projection_matrix, preferred_element_type=jnp.float32)
    value_part = jnp.dot(scaled, value_projection_matrix, preferred_element_type=jnp.float32)
    down_row_count = adapter_down_matrix.shape[0]
    resident_down_map = adapter_choice_index - head_index * down_row_count
    down_owned = (resident_down_map >= 0) & (resident_down_map < down_row_count)
    down_map_rows = adapter_down_matrix[jnp.clip(resident_down_map, 0, down_row_count - 1)]
    down_part = jnp.einsum("by,bey->be", scaled, down_map_rows, preferred_element_type=jnp.float32)
    down_part = jnp.where(down_owned[:, None], down_part, 0.0)
    square_sum = lax.psum(square_part, "seq")
    down_total_sum = lax.psum(down_part, ("seq", "head"))
    inverse_factor = lax.rsqrt(square_sum / model_width + norm_epsilon)
    reduced_rank_state = (down_total_sum * inverse_factor[:, None] * adapter_scale_factor).astype(
        jnp.bfloat16
    )
    up_row_count = adapter_up_matrix.shape[0]
    resident_up_map = adapter_choice_index - seq_index * up_row_count
    up_owned = (resident_up_map >= 0) & (resident_up_map < up_row_count)
    up_map_rows = adapter_up_matrix[jnp.clip(resident_up_map, 0, up_row_count - 1)]
    expand = jnp.einsum(
        "rk,rkc->rc", reduced_rank_state, up_map_rows, preferred_element_type=jnp.float32
    )
    expand = jnp.where(up_owned[:, None], expand, 0.0)
    query_sum, key_sum, value_sum = lax.psum((query_part, key_part, value_part), "seq")
    up_sum = lax.psum(expand, "seq")
    query_full = query_sum * inverse_factor[:, None] + up_sum
    key_new = key_sum * inverse_factor[:, None]
    value_new = value_sum * inverse_factor[:, None]
    query_rot = rotate(query_full.reshape(requests, heads_local, head_dim), lengths).astype(
        jnp.bfloat16
    )
    key_rot = rotate(key_new.reshape(requests, kv_local, head_dim), lengths).astype(jnp.bfloat16)
    value_own = value_new.reshape(requests, kv_local, head_dim).astype(jnp.bfloat16)
    grouped = query_rot.reshape(requests, kv_local, group_size, head_dim)
    score_scale = head_dim ** (-0.5)
    scores = (
        jnp.einsum(
            "rhgd,rjhd->rhgj", grouped, rotated_key_cache, preferred_element_type=jnp.float32
        )
        * score_scale
    )
    position = seq_index * cached + jnp.arange(cached, dtype=jnp.int32)
    valid_mask = (position[None, :] < lengths[:, None])[:, None, None, :]
    scores = jnp.where(valid_mask, scores, masked_score)
    local_max = jnp.max(scores, axis=-1)
    weights = jnp.where(valid_mask, jnp.exp(scores - local_max[..., None]), 0.0)
    local_total = jnp.sum(weights, axis=-1)
    local_out = jnp.einsum(
        "rhgj,rjhd->rhgd",
        weights.astype(jnp.bfloat16),
        cached_value_rows,
        preferred_element_type=jnp.float32,
    )
    own_score = (
        jnp.einsum("rhgd,rhd->rhg", grouped, key_rot, preferred_element_type=jnp.float32)
        * score_scale
    )
    own_value = value_own.astype(jnp.float32)[:, :, None, :]
    whole_max, total_sum, out_sum = joined(
        (local_max, local_total, local_out), "seq", combine_parts
    )
    overall = jnp.maximum(whole_max, own_score)
    factor = jnp.exp(whole_max - overall)
    own_weight = jnp.exp(own_score - overall)
    denominator = total_sum * factor + own_weight
    summed = out_sum * factor[..., None] + own_weight[..., None] * own_value
    attended = (summed / denominator[..., None]).reshape(requests, query_cols).astype(jnp.bfloat16)
    out_part = jnp.dot(attended, output_projection_matrix, preferred_element_type=jnp.float32)
    output_sum = lax.psum(out_part, "head")
    return output_sum.astype(jnp.bfloat16)


def solution(mesh):
    return jax.shard_map(
        body,
        mesh=mesh,
        in_specs=(
            P(None, "seq"),
            P("seq"),
            P("seq", "head"),
            P("seq", "head"),
            P("seq", "head"),
            P("head", "seq"),
            P("head", None, "seq"),
            P("seq", None, "head"),
            P(),
            P(),
            P(None, "seq", "head", None),
            P(None, "seq", "head", None),
        ),
        out_specs=P(None, "seq"),
        check_vma=False,
    )
```

profile of v0, /device:TPU:0, one launch (start us, length us, event | category | flops | bytes accessed | tf_op | source)
XLA Modules:
  0.0 359.2 jit_solution(16942962963859479720)
XLA Ops:
  7.3 1.3 fusion.28
  8.6 1.5 fusion.40
  10.2 1.9 fusion.38
  14.1 2.8 gather_fusion
  17.1 42.0 %psum.51 = f32[16,16]{1,0:T(8,128)S(1)} all-reduce(f32[16,16]{1,0:T(8,128)S(1)} %broadcast_select_fusion), channel_id=1, replica_groups=mesh['seq'=16,'head'=2] {'seq','head'}, use_global_device_ids=true, to_apply=%region_3.4 | all-reduce | flops 256 | bytes 2048 | tf_op jit(solution)/shard_map/psum | solution.py:94
  59.1 3.6 fusion.43
  62.7 2.9 gather_fusion.1
  65.6 56.4 %all-reduce.5.cloned.1.call-done = (f32[16]{0:T(128)}, f32[16,512]{1,0:T(8,128)}, f32[16,512]{1,0:T(8,128)}) async-done(((f32[16]{0:T(128)}, f32[16,512]{1,0:T(8,128)}, f32[16,512]{1,0:T(8,128)}), (f32[16]{0:T(128)}, f32[16,512]{1,0:T(8,128)}, f32[16,512]{1,0:T(8,128)})) %all-reduce.5.cloned.1.call-update) | async-done | bytes 65616 | tf_op jit(solution)/shard_map/psum | solution.py:93
  124.4 112.1 %all-reduce.7.cloned.1.call-done = (f32[16,4096]{1,0:T(8,128)}, f32[16,4096]{1,0:T(8,128)}) async-done(((f32[16,4096]{1,0:T(8,128)}, f32[16,4096]{1,0:T(8,128)}), (f32[16,4096]{1,0:T(8,128)}, f32[16,4096]{1,0:T(8,128)})) %all-reduce.7.cloned.1.call-update) | async-done | bytes 524304 | tf_op jit(solution)/shard_map/psum | solution.py:108
  236.5 1.3 add_bitcast_fusion
  238.0 3.5 fusion.52
  241.5 1.4 fusion.13
  243.6 40.8 %all-gather = bf16[256,4,8]{2,1,0:T(4,128)(2,1)S(1)} all-gather(bf16[16,4,8]{2,1,0:T(4,128)(2,1)S(1)} %convert_element_type.140), channel_id=2, replica_groups=mesh['seq'=16,'head'=2] {'seq'}, dimensions={0}, use_global_device_ids=true | all-gather | bytes 17408 | tf_op jit(solution)/shard_map/all_gather | solution.py:14
  285.0 38.2 %all-gather.1 = bf16[256,4,8]{2,1,0:T(4,128)(2,1)S(1)} all-gather(bf16[16,4,8]{2,1,0:T(4,128)(2,1)S(1)} %fusion.17), channel_id=3, replica_groups=mesh['seq'=16,'head'=2] {'seq'}, dimensions={0}, use_global_device_ids=true | all-gather | bytes 17408 | tf_op jit(solution)/shard_map/all_gather | solution.py:14
  324.5 20.8 %while.19 = (s32[]{:T(128)}, f32[16,4,8]{0,2,1:T(8,128)S(1)}, f32[16,4,8]{0,2,1:T(8,128)S(1)}, f32[16,4,8,128]{3,2,1,0:T(8,128)S(1)}, bf16[16,16,4,8]{1,3,2,0:T(...) while((s32[]{:T(128)}, f32[16,4,8]{0,2,1:T(8,128)S(1)}, ...), condition=%wide.region_8.9_spmd, body=%wide.region_7.8_spmd.sunk | while | flops 266245 | bytes 682127 | solution.py:22
  324.7 1.2 fusion.62
  327.5 1.2 fusion.62
  328.9 1.2 fusion.62
  331.6 1.2 fusion.62
  334.4 1.2 fusion.62
  337.2 1.2 fusion.62
  338.6 1.2 fusion.62
  345.8 2.8 fusion.24
  348.7 4.0 %psum.55 = bf16[16,512]{1,0:T(8,128)(2,1)} all-reduce(f32[16,512]{1,0:T(8,128)S(1)} %fusion.24), channel_id=1, replica_groups=mesh['seq'=16,'head'=2] {'head'}, use_global_device_ids=true, to_apply=%region_11.12 | all-reduce | flops 8192 | bytes 49152 | tf_op jit(solution)/shard_map/psum | solution.py:152
  (109 shorter events, 20.7 us)
Async XLA Ops:
  6.5 2.1 copy-start
  6.5 115.5 %all-reduce.5.cloned.1.call-start = ((), (), s32[]{:S(2)}) async-start(), calls=%async_computation.1 | async-start | bytes 132096 | tf_op jit(solution)/shard_map/psum | solution.py:93
  12.0 224.4 %all-reduce.7.cloned.1.call-start = ((), (), s32[]{:S(2)}) async-start(), calls=%async_computation.2 | async-start | bytes 1048576 | tf_op jit(solution)/shard_map/psum | solution.py:108
  62.7 61.5 %copy-start.3 = (s32[16]{0:T(128)S(1)}, s32[16]{0:T(128)}, u32[]{:S(2)}) copy-start(s32[16]{0:T(128)} %param.23) | copy-start | bytes 196
  124.1 199.4 %all-gather.5.cloned.1.call-start = ((), (), s32[]{:S(2)}) async-start(), calls=%async_computation | async-start | bytes 2228224 | tf_op jit(solution)/shard_map/all_gather | solution.py:14
  236.5 5.0 %copy-start.4 = (bf16[16,256,4,128]{3,2,1,0:T(4,128)(2,1)S(1)}, bf16[16,256,4,128]{3,2,1,0:T(4,128)(2,1)}, u32[]{:S(2)}) copy-start(bf16[16,256,4,128]{3,2,1,0:T(4,128)(2,1)} %param.25) | copy-start | bytes 12582916
  237.9 5.0 %copy-start.1 = (f32[16,512]{1,0:T(8,128)S(1)}, f32[16,512]{1,0:T(8,128)}, u32[]{:S(2)}) copy-start(f32[16,512]{1,0:T(8,128)} %get-tuple-element.215) | copy-start | bytes 98308
  238.0 5.0 %copy-start.2 = (f32[16,512]{1,0:T(8,128)S(1)}, f32[16,512]{1,0:T(8,128)}, u32[]{:S(2)}) copy-start(f32[16,512]{1,0:T(8,128)} %get-tuple-element.216) | copy-start | bytes 98308
Sparse Core Ops, SparseCore 0:
  13.2 108.7 all-reduce.4
  127.2 109.2 all-reduce.6
  243.0 61.0 all-gather.4
where the time goes:
time: 360 us; the launch traced here: 359 us
  waiting for transfers between devices  169 us (47%)
  blocking collectives  125 us (35%)
  other arithmetic  27.1 us (8%)
  matrix products  15.6 us (4%)
  between operations  13.3 us (4%)
  local copies, waits for them, and re-layouts  8.98 us (2%)
    psum x1, waiting for transfers between devices, body(): up_sum = lax.psum(expand, 'seq')  112 us
    all_gather x2, blocking collectives, joined(): lax.all_gather(part.astype(kind), axis)  79.1 us
    psum x1, waiting for transfers between devices, body(): square_sum = lax.psum(square_part, 'seq')  56.4 us
    psum x1, blocking collectives, body(): down_total_sum = lax.psum(down_part, ('seq', 'head'))  42 us
    add x15, other arithmetic, combine_parts(): out_one * scale_one[..., None] + out_two * scale_two[..., None]  17.6 us
  transfers between devices with their start and end apart: 3, of which 2 were waited for; matrix products, arithmetic and copies ran while one was open for 4% of the time, Pallas kernels for 0%

commit v1 on v0

v1 whole, which is shorter than its diff:
```python
import jax
import jax.numpy as jnp
from jax import lax
from jax.sharding import PartitionSpec as P

norm_epsilon = 1e-05
adapter_scale_factor = 1.0
rope_base = 500000.0
masked_score = -1e30


def exchanged(parts):
    return lax.all_to_all(parts, "seq", 0, 0, tiled=True)


def spread(value):
    return exchanged(jnp.broadcast_to(value[None], (lax.axis_size("seq"),) + value.shape))


def narrow(value):
    return lax.reduce_precision(value, exponent_bits=8, mantissa_bits=7)


def rotate(vectors, cosine, sine_val):
    half_dim = vectors.shape[-1] // 2
    lower_half = vectors[..., :half_dim]
    upper_half = vectors[..., half_dim:]
    return jnp.concatenate(
        [lower_half * cosine - upper_half * sine_val, upper_half * cosine + lower_half * sine_val],
        axis=-1,
    )


def angle_tables(positions, half_dim):
    frequency = jnp.exp(
        -jnp.arange(half_dim, dtype=jnp.float32) * (jnp.log(jnp.float32(rope_base)) / half_dim)
    )
    angles = positions.astype(jnp.float32)[:, None] * frequency[None, :]
    return jnp.cos(angles), jnp.sin(angles)


def body(
    hidden_state_input,
    attention_norm_gain,
    query_projection_matrix,
    key_projection_matrix,
    value_projection_matrix,
    output_projection_matrix,
    adapter_down_matrix,
    adapter_up_matrix,
    adapter_choice_index,
    lengths,
    rotated_key_cache,
    cached_value_rows,
):
    requests = hidden_state_input.shape[0]
    width_part = hidden_state_input.shape[1]
    cached = rotated_key_cache.shape[1]
    kv_local = rotated_key_cache.shape[2]
    head_dim = rotated_key_cache.shape[3]
    query_cols = query_projection_matrix.shape[1]
    heads_local = query_cols // head_dim
    group_size = heads_local // kv_local
    rank = adapter_down_matrix.shape[1]
    seq_index = lax.axis_index("seq")
    head_index = lax.axis_index("head")
    seq_size = lax.axis_size("seq")
    head_size = lax.axis_size("head")
    model_width = width_part * seq_size
    score_scale = head_dim ** (-0.5)
    own_rows = requests * heads_local // seq_size
    if own_rows % group_size == 0:
        own_kv, kv_repeat = own_rows // group_size, 1
    else:
        own_kv, kv_repeat = 1, group_size // own_rows

    values32 = hidden_state_input.astype(jnp.float32)
    square_part = jnp.sum(values32 * values32, axis=1)
    square_part = jnp.where(head_index == 0, square_part, 0.0)
    scaled = (values32 * attention_norm_gain.astype(jnp.float32)[None, :]).astype(jnp.bfloat16)
    down_row_count = adapter_down_matrix.shape[0]
    resident_down_map = adapter_choice_index - head_index * down_row_count
    down_owned = (resident_down_map >= 0) & (resident_down_map < down_row_count)
    down_map_rows = adapter_down_matrix[jnp.clip(resident_down_map, 0, down_row_count - 1)]
    down_part = jnp.einsum("by,bey->be", scaled, down_map_rows, preferred_element_type=jnp.float32)
    down_part = jnp.where(down_owned[:, None], down_part, 0.0)

    small = jnp.concatenate([down_part.reshape(-1), square_part])
    small = jnp.pad(small, (0, -small.shape[0] % 128))
    everyone = seq_size * head_size
    small = lax.all_to_all(
        jnp.broadcast_to(small[None], (everyone,) + small.shape), ("seq", "head"), 0, 0, tiled=True
    )
    small = jnp.sum(small, axis=0)
    down_total_sum = small[: requests * rank].reshape(requests, rank)
    square_sum = small[requests * rank : requests * rank + requests]
    inverse_factor = lax.rsqrt(square_sum / model_width + norm_epsilon)
    reduced_rank_state = (down_total_sum * inverse_factor[:, None] * adapter_scale_factor).astype(
        jnp.bfloat16
    )

    up_row_count = adapter_up_matrix.shape[0]
    resident_up_map = adapter_choice_index - seq_index * up_row_count
    up_owned = (resident_up_map >= 0) & (resident_up_map < up_row_count)
    up_map_rows = adapter_up_matrix[jnp.clip(resident_up_map, 0, up_row_count - 1)]
    expand = jnp.einsum(
        "rk,rkc->rc", reduced_rank_state, up_map_rows, preferred_element_type=jnp.float32
    )
    expand = jnp.where(up_owned[:, None], expand, 0.0)
    query_part = jnp.dot(scaled, query_projection_matrix, preferred_element_type=jnp.float32)
    key_part = jnp.dot(scaled, key_projection_matrix, preferred_element_type=jnp.float32)
    value_part = jnp.dot(scaled, value_projection_matrix, preferred_element_type=jnp.float32)
    query_part = query_part * inverse_factor[:, None] + expand
    key_part = key_part * inverse_factor[:, None]
    value_part = value_part * inverse_factor[:, None]

    def kv_parts(part):
        rows = part.astype(jnp.bfloat16).reshape(-1, head_dim)
        return jnp.repeat(rows, kv_repeat, axis=0).reshape(seq_size, own_kv, head_dim)

    sums = exchanged(
        jnp.concatenate(
            [
                query_part.astype(jnp.bfloat16).reshape(seq_size, own_rows, head_dim),
                kv_parts(key_part),
                kv_parts(value_part),
            ],
            axis=1,
        )
    )
    sums = jnp.sum(sums.astype(jnp.float32), axis=0)
    query_row_request = (seq_index * own_rows + jnp.arange(own_rows)) // heads_local
    kv_row_request = query_row_request.reshape(own_kv, -1)[:, 0]
    cosine, sine_val = angle_tables(lengths[query_row_request], head_dim // 2)
    query_rot = rotate(sums[:own_rows], cosine, sine_val).astype(jnp.bfloat16)
    cosine, sine_val = angle_tables(lengths[kv_row_request], head_dim // 2)
    key_rot = rotate(sums[own_rows : own_rows + own_kv], cosine, sine_val).astype(jnp.bfloat16)
    value_own = sums[own_rows + own_kv :].astype(jnp.bfloat16)

    grouped = spread(query_rot).reshape(requests, kv_local, group_size, head_dim)
    scores = (
        jnp.einsum(
            "rhgd,rjhd->rhgj", grouped, rotated_key_cache, preferred_element_type=jnp.float32
        )
        * score_scale
    )
    position = seq_index * cached + jnp.arange(cached, dtype=jnp.int32)
    valid_mask = (position[None, :] < lengths[:, None])[:, None, None, :]
    scores = jnp.where(valid_mask, scores, masked_score)
    local_max = jnp.max(scores, axis=-1)
    shift_high = narrow(local_max)
    shift_low = narrow(local_max - shift_high)
    shift = shift_high + shift_low
    weights = jnp.where(valid_mask, jnp.exp(scores - shift[..., None]), 0.0)
    local_total = jnp.sum(weights, axis=-1)
    total_high = narrow(local_total)
    total_low = narrow(local_total - total_high)
    local_out = jnp.einsum(
        "rhgj,rjhd->rhgd",
        weights.astype(jnp.bfloat16),
        cached_value_rows,
        preferred_element_type=jnp.float32,
    )
    stats = jnp.stack(
        [
            piece.reshape(seq_size, own_rows)
            for piece in (shift_high, shift_low, total_high, total_low)
        ],
        axis=1,
    ).reshape(seq_size, 4 * own_rows)
    stats = jnp.pad(stats, ((0, 0), (0, -stats.shape[1] % head_dim)))
    stat_rows = stats.shape[1] // head_dim
    parts = exchanged(
        jnp.concatenate(
            [
                local_out.astype(jnp.bfloat16).reshape(seq_size, own_rows, head_dim),
                stats.astype(jnp.bfloat16).reshape(seq_size, stat_rows, head_dim),
            ],
            axis=1,
        )
    ).astype(jnp.float32)
    outs = parts[:, :own_rows]
    stats = parts[:, own_rows:].reshape(seq_size, -1)[:, : 4 * own_rows]
    stats = stats.reshape(seq_size, 4, own_rows)
    shifts = stats[:, 0] + stats[:, 1]
    totals = stats[:, 2] + stats[:, 3]

    own_group = own_rows // own_kv
    query_own = query_rot.astype(jnp.float32).reshape(own_kv, own_group, head_dim)
    own_score = jnp.sum(query_own * key_rot.astype(jnp.float32)[:, None, :], axis=-1) * score_scale
    own_score = own_score.reshape(own_rows)
    overall = jnp.maximum(jnp.max(shifts, axis=0), own_score)
    factor = jnp.exp(shifts - overall[None, :])
    own_weight = jnp.exp(own_score - overall)
    denominator = jnp.sum(totals * factor, axis=0) + own_weight
    own_value = jnp.broadcast_to(
        value_own.astype(jnp.float32)[:, None, :], (own_kv, own_group, head_dim)
    ).reshape(own_rows, head_dim)
    summed = jnp.sum(outs * factor[..., None], axis=0) + own_weight[:, None] * own_value
    attended = (summed / denominator[:, None]).astype(jnp.bfloat16)

    attended = spread(attended).reshape(requests, query_cols)
    out_part = jnp.dot(attended, output_projection_matrix, preferred_element_type=jnp.float32)
    if head_size == 2:
        output_sum = out_part + lax.ppermute(out_part, "head", [(0, 1), (1, 0)])
    else:
        output_sum = lax.psum(out_part, "head")
    return output_sum.astype(jnp.bfloat16)


def solution(mesh):
    return jax.shard_map(
        body,
        mesh=mesh,
        in_specs=(
            P(None, "seq"),
            P("seq"),
            P("seq", "head"),
            P("seq", "head"),
            P("seq", "head"),
            P("head", "seq"),
            P("head", None, "seq"),
            P("seq", None, "head"),
            P(),
            P(),
            P(None, "seq", "head", None),
            P(None, "seq", "head", None),
        ),
        out_specs=P(None, "seq"),
        check_vma=False,
    )
```

time: 360 us -> 87.3 us (0.24)
  waiting for transfers between devices: 169 us -> 26.1 us
  blocking collectives: 125 us -> 10.6 us
  other arithmetic: 27.1 us -> 6.63 us
  starting transfers between devices: 0.09 us -> 19.5 us
  between operations: 13.3 us -> 0.29 us
    psum x2 -> x0, waiting for transfers between devices: 168 us -> none  [the longest x1 112 us: body(): up_sum = lax.psum(expand, 'seq')]
    all_gather x2 -> x0, blocking collectives: 79.1 us -> none  [joined(): lax.all_gather(part.astype(kind), axis)]
    psum x2 -> x0, blocking collectives: 46 us -> none  [the longest x1 42 us: body(): down_total_sum = lax.psum(down_part, ('seq', 'head'))]
    all_to_all x0 -> x4, waiting for transfers between devices: none -> 24.9 us  [the longest x3 23.2 us: exchanged(): return lax.all_to_all(parts, 'seq', 0, 0, tiled=True)]
    all_to_all x0 -> x4, starting transfers between devices: none -> 19.5 us  [the longest x3 12.2 us: exchanged(): return lax.all_to_all(parts, 'seq', 0, 0, tiled=True)]
    add x31 -> x2, other arithmetic: 18 us -> 0.02 us  [the longest x1 0.01 us: body(): shift = shift_high + shift_low]
    all_to_all x0 -> x1, blocking collectives: none -> 10.6 us  [exchanged(): return lax.all_to_all(parts, 'seq', 0, 0, tiled=True)]
  transfers between devices with their start and end apart: 3 -> 5, of which waited for: 2 -> 5; matrix products, arithmetic and copies ran while one was open for 4% -> 7% of each run, Pallas kernels for 0% -> 0%
where the time goes in v1:
time: 87.3 us; the launch traced here: 86.5 us
  waiting for transfers between devices  26.1 us (30%)
  starting transfers between devices  19.5 us (22%)
  matrix products  12.9 us (15%)
  blocking collectives  10.6 us (12%)
  local copies, waits for them, and re-layouts  10.4 us (12%)
  other arithmetic  6.63 us (8%)
    all_to_all x3, waiting for transfers between devices, exchanged(): return lax.all_to_all(parts, 'seq', 0, 0, tiled=True)  23.2 us
    all_to_all x3, starting transfers between devices, exchanged(): return lax.all_to_all(parts, 'seq', 0, 0, tiled=True)  12.2 us
    all_to_all x1, blocking collectives, exchanged(): return lax.all_to_all(parts, 'seq', 0, 0, tiled=True)  10.6 us
    all_to_all x1, starting transfers between devices, body(): lax.all_to_all(jnp.broadcast_to(small[None], (everyone,) + small.shape),...  7.33 us
    dot_general x1, matrix products, body(): jnp.einsum('rhgd,rjhd->rhgj', grouped, rotated_key_cache, preferred_eleme...  3.46 us
    dot_general x1, matrix products, body(): jnp.einsum('rhgj,rjhd->rhgd', weights.astype(jnp.bfloat16), cached_value_...  2.9 us
    gather x1, local copies, waits for them, and re-layouts, body(): adapter_up_matrix[jnp.clip(resident_up_map, 0, up_row_count - 1)]  2.88 us
    dot_general x1, matrix products, body(): jnp.dot(scaled, query_projection_matrix, preferred_element_type=jnp.float32)  2.86 us
  transfers between devices with their start and end apart: 5, of which 5 were waited for; matrix products, arithmetic and copies ran while one was open for 7% of the time, Pallas kernels for 0%

profile of v1, /device:TPU:0, one launch (start us, length us, event | category | flops | bytes accessed | tf_op | source)
XLA Modules:
  0.0 86.5 jit_solution(1372069756960309032)
XLA Ops:
  0.0 0.7 compare_select_fusion.2
  1.4 0.7 convert_element_type.97
  2.1 2.7 %gather_fusion = bf16[16,16,512]{2,1,0:T(8,128)(2,1)S(1)} fusion(bf16[256,16,512]{2,1,0:T(8,128)(2,1)} %param.18, s32[1024]{0:T(1024)S(1)} %pad_clamp_fusion.3), kind=kCustom, calls=%fused_computation | custom fusion | bytes 524352 | tf_op jit(solution)/shard_map/gather | solution.py:84
  4.8 0.9 %fusion.57 = (bf16[16,512,1]{1,0,2:T(8,128)(2,1)S(1)}, f32[16]{0:T(128)S(1)}) fusion(f32[512]{0:T(512)S(1)} %convert_element_type.97, bf16[16,512]{1,0:T(8,128)(2,1)} %param.12), kind=kLoop, calls=%fused_computation.80 | loop fusion | flops 40944 | bytes 34880 | tf_op jit(solution)/shard_map/convert_element_type | solution.py:80
  6.8 7.3 %all-to-all-start = ((f32[32,1,384]{2,1,0:T(1,128)}), f32[32,1,384]{2,1,0:T(1,128)S(1)}, u32[]{:S(2)}, u32[]{:S(2)}) async-start(f32[32,1,384]{2,1,0:T(1,128)} %broadcast_in_dim.63), calls=%async_computation | async-start | bytes 98304 | tf_op jit(solution)/shard_map/all_to_all | solution.py:91
  14.2 1.3 %gather_fusion.3 = s32[4]{0:T(128)S(1)} fusion(s32[16]{0:T(128)} %param.21, s32[1024]{0:T(1024)S(1)} %pad_clamp_fusion), kind=kCustom, calls=%fused_computation.3 | custom fusion | bytes 48 | tf_op jit(solution)/shard_map/gather | solution.py:136
  15.5 1.4 %gather_fusion.2 = s32[32]{0:T(128)S(1)} fusion(s32[16]{0:T(128)} %param.21, s32[1024]{0:T(1024)S(1)} %pad_clamp_fusion.1), kind=kCustom, calls=%fused_computation.2 | custom fusion | bytes 384 | tf_op jit(solution)/shard_map/gather | solution.py:134
  16.8 2.9 %gather_fusion.1 = bf16[16,16,4096]{2,1,0:T(8,128)(2,1)S(1)} fusion(bf16[32,16,4096]{2,1,0:T(8,128)(2,1)} %param.19, s32[1024]{0:T(1024)S(1)} %pad_clamp_fusion.2), kind=kCustom, calls=%fused_computation.1 | custom fusion | bytes 4194368 | tf_op jit(solution)/shard_map/gather | solution.py:105
  19.8 1.7 %all-to-all-done = f32[32,1,384]{2,1,0:T(1,128)S(1)} async-done(((f32[32,1,384]{2,1,0:T(1,128)}), f32[32,1,384]{2,1,0:T(1,128)S(1)}, u32[]{:S(2)}, u32[]{:S(2)}) %all-to-all-start) | async-done | bytes 49184 | tf_op jit(solution)/shard_map/all_to_all | solution.py:91
  22.1 2.9 %fusion.18 = bf16[2,8,32,128]{3,1,2,0:T(8,128)(2,1)S(1)} fusion(bf16[512,4096]{1,0:T(8,128)(2,1)} %param.14, f32[16,1,4096]{2,1,0:T(1,128)S(1)} %fusion.53, f32[16]{0:T(128)S(1)} %add_rsqrt_fusion, pred[16]{0:T(512)(128)(4,1)S(1)} %get-tuple-element.22, bf16[16,512]{1,0:T(8,128)(2,1)S(1)} %copy-done.3, f32[512]{0:T(512)S(1)} %convert_element_type.97), kind=kOutput, calls=%fused_computation.15 | convolution fusion | flops 67395584 | bytes 4606032 | tf_op jit(solution)/shard_map/dot_general | solution.py:110
  25.4 0.7 pad_maximum_fusion
  26.1 5.2 %all-to-all-start.1 = ((bf16[16,40,128]{2,1,0:T(8,128)(2,1)}), bf16[16,40,128]{2,1,0:T(8,128)(2,1)S(1)}, u32[]{:S(2)}, u32[]{:S(2)}) async-start(bf16[16,40,128]{2,1,0:T(8,128)(2,1)} %pad_maximum_fusion), calls=%async_computation.1 | async-start | bytes 327680 | tf_op jit(solution)/shard_map/all_to_all | solution.py:13
  31.4 8.0 %all-to-all-done.1 = bf16[16,40,128]{2,1,0:T(8,128)(2,1)S(1)} async-done(((bf16[16,40,128]{2,1,0:T(8,128)(2,1)}), bf16[16,40,128]{2,1,0:T(8,128)(2,1)S(1)}, u32[]{:S(2)}, u32[]{:S(2)}) %all-to-all-start.1) | async-done | bytes 163872 | tf_op jit(solution)/shard_map/all_to_all | solution.py:13
  39.7 0.7 broadcast_in_dim.107
  40.3 3.5 %all-to-all-start.2 = ((bf16[16,32,128]{2,1,0:T(8,128)(2,1)}), bf16[16,32,128]{2,1,0:T(8,128)(2,1)S(1)}, u32[]{:S(2)}, u32[]{:S(2)}) async-start(bf16[16,32,128]{2,1,0:T(8,128)(2,1)} %broadcast_in_dim.107), calls=%async_computation.2 | async-start | bytes 262144 | tf_op jit(solution)/shard_map/all_to_all | solution.py:13
  44.2 7.4 %all-to-all-done.2 = bf16[16,32,128]{2,1,0:T(8,128)(2,1)S(1)} async-done(((bf16[16,32,128]{2,1,0:T(8,128)(2,1)}), bf16[16,32,128]{2,1,0:T(8,128)(2,1)S(1)}, u32[]{:S(2)}, u32[]{:S(2)}) %all-to-all-start.2) | async-done | bytes 131104 | tf_op jit(solution)/shard_map/all_to_all | solution.py:13
  51.6 3.5 %fusion.78 = (f32[16,4,8]{2,1,0:T(4,128)S(1)}, f32[16,4,8,256]{3,2,1,0:T(8,128)S(1)}) fusion(bf16[16,256,4,128]{3,2,1,0:T(4,128)(2,1)} %param.22, bf16[16,32,128]{2,1,0:T(8,128)(2,1)S(1)} %all-to-all-done.2, pred[16,256]{1,0:T(8,128)(4,1)S(1)} %broadcast_compare_fusion), kind=kOutput, calls=%fused_computation.133 | convolution fusion | flops 33947136 | bytes 4855808 | tf_op jit(solution)/shard_map/rhgd,rjhd->rhgj/dot_general | solution.py:142
  55.6 2.9 %fusion.15 = bf16[16,32,128]{2,1,0:T(8,128)(2,1)S(1)} fusion(bf16[16,256,4,128]{3,2,1,0:T(4,128)(2,1)} %param.23, f32[16,4,8,256]{3,2,1,0:T(8,128)S(1)} %get-tuple-element.27, f32[16,4,8]{2,1,0:T(4,128)S(1)} %copy.54, pred[16,256]{1,0:T(8,128)(4,1)S(1)} %broadcast_compare_fusion), kind=kOutput, calls=%fused_computation.14 | convolution fusion | flops 34013184 | bytes 4855808 | tf_op jit(solution)/shard_map/rhgj,rjhd->rhgd/dot_general | solution.py:158
  58.7 0.7 pad_maximum_fusion.1
  59.4 3.5 %all-to-all-start.3 = ((bf16[16,33,128]{2,1,0:T(8,128)(2,1)}), bf16[16,33,128]{2,1,0:T(8,128)(2,1)S(1)}, u32[]{:S(2)}, u32[]{:S(2)}) async-start(bf16[16,33,128]{2,1,0:T(8,128)(2,1)} %pad_maximum_fusion.1), calls=%async_computation.3 | async-start | bytes 327680 | tf_op jit(solution)/shard_map/all_to_all | solution.py:13
  63.0 7.8 %all-to-all-done.3 = bf16[16,33,128]{2,1,0:T(8,128)(2,1)S(1)} async-done(((bf16[16,33,128]{2,1,0:T(8,128)(2,1)}), bf16[16,33,128]{2,1,0:T(8,128)(2,1)S(1)}, u32[]{:S(2)}, u32[]{:S(2)}) %all-to-all-start.3) | async-done | bytes 135200 | tf_op jit(solution)/shard_map/all_to_all | solution.py:13
  71.3 10.6 %all_to_all.26 = bf16[16,32,128]{2,1,0:T(8,128)(2,1)S(1)} all-to-all(bf16[16,32,128]{2,1,0:T(8,128)(2,1)S(1)} %broadcast_in_dim.111), channel_id=1, replica_groups=mesh['seq'=16,'head'=2] {'seq'}, dimensions={0} | all-to-all | bytes 262144 | tf_op jit(solution)/shard_map/all_to_all | solution.py:13
  81.9 2.8 %fusion.28 = f32[16,512]{1,0:T(8,128)S(1)} fusion(bf16[4096,512]{1,0:T(8,128)(2,1)} %param.17, bf16[2,8,32,128]{3,2,1,0:T(8,128)(2,1)S(1)} %bitcast.59), kind=kOutput, calls=%fused_computation.32 | convolution fusion | flops 67108864 | bytes 4358144 | tf_op jit(solution)/shard_map/dot_general | solution.py:203
  84.7 1.2 %collective-permute-done = f32[16,512]{1,0:T(8,128)S(1)} collective-permute-done((f32[16,512]{1,0:T(8,128)S(1)}, f32[16,512]{1,0:T(8,128)S(1)}, u32[]{:S(2)}, u32[]{:S(2)}) %collective-permute-start) | collective-permute-done | bytes 32800 | tf_op jit(solution)/shard_map/ppermute | solution.py:205
  (68 shorter events, 5.3 us)
Async XLA Ops:
  0.0 25.0 %copy-start = (bf16[512,512]{1,0:T(8,128)(2,1)S(1)}, bf16[512,512]{1,0:T(8,128)(2,1)}, u32[]{:S(2)}) copy-start(bf16[512,512]{1,0:T(8,128)(2,1)} %param.15) | copy-start | bytes 1572868
  4.8 17.3 %copy-start.3 = (bf16[16,512]{1,0:T(8,128)(2,1)S(1)}, bf16[16,512]{1,0:T(8,128)(2,1)}, u32[]{:S(2)}) copy-start(bf16[16,512]{1,0:T(8,128)(2,1)} %param.12) | copy-start | bytes 49156
  6.8 14.7 %all-to-all-start = ((f32[32,1,384]{2,1,0:T(1,128)}), f32[32,1,384]{2,1,0:T(1,128)S(1)}, u32[]{:S(2)}, u32[]{:S(2)}) async-start(f32[32,1,384]{2,1,0:T(1,128)} %broadcast_in_dim.63), calls=%async_computation | async-start | bytes 98304 | tf_op jit(solution)/shard_map/all_to_all | solution.py:91
  19.7 5.5 %copy-start.2 = (bf16[512,512]{1,0:T(8,128)(2,1)S(1)}, bf16[512,512]{1,0:T(8,128)(2,1)}, u32[]{:S(2)}) copy-start(bf16[512,512]{1,0:T(8,128)(2,1)} %param.16) | copy-start | bytes 1572868
  21.7 9.7 %copy-start.1 = (s32[16]{0:T(128)S(1)}, s32[16]{0:T(128)}, u32[]{:S(2)}) copy-start(s32[16]{0:T(128)} %param.21) | copy-start | bytes 196
  26.1 13.3 %all-to-all-start.1 = ((bf16[16,40,128]{2,1,0:T(8,128)(2,1)}), bf16[16,40,128]{2,1,0:T(8,128)(2,1)S(1)}, u32[]{:S(2)}, u32[]{:S(2)}) async-start(bf16[16,40,128]{2,1,0:T(8,128)(2,1)} %pad_maximum_fusion), calls=%async_computation.1 | async-start | bytes 327680 | tf_op jit(solution)/shard_map/all_to_all | solution.py:13
  40.3 11.3 %all-to-all-start.2 = ((bf16[16,32,128]{2,1,0:T(8,128)(2,1)}), bf16[16,32,128]{2,1,0:T(8,128)(2,1)S(1)}, u32[]{:S(2)}, u32[]{:S(2)}) async-start(bf16[16,32,128]{2,1,0:T(8,128)(2,1)} %broadcast_in_dim.107), calls=%async_computation.2 | async-start | bytes 262144 | tf_op jit(solution)/shard_map/all_to_all | solution.py:13
  59.4 11.4 %all-to-all-start.3 = ((bf16[16,33,128]{2,1,0:T(8,128)(2,1)}), bf16[16,33,128]{2,1,0:T(8,128)(2,1)S(1)}, u32[]{:S(2)}, u32[]{:S(2)}) async-start(bf16[16,33,128]{2,1,0:T(8,128)(2,1)} %pad_maximum_fusion.1), calls=%async_computation.3 | async-start | bytes 327680 | tf_op jit(solution)/shard_map/all_to_all | solution.py:13
  84.7 1.2 %collective-permute-start = (f32[16,512]{1,0:T(8,128)S(1)}, f32[16,512]{1,0:T(8,128)S(1)}, u32[]{:S(2)}, u32[]{:S(2)}) collective-permute-start(f32[16,512]{1,0:T(8,128)S(1)} %fusion.28), channel_id=1, source_target_pairs={{0,1},{1,0},{2,3},{3,2},{4,5},{5,4},{6,7},{7,6},{8,9},{9,8},{10,11... | collective-permute-start | bytes 98312 | tf_op jit(solution)/shard_map/ppermute | solution.py:205

commit v2 on v0

v2 whole, which is shorter than its diff:
```python
import functools
import math

import jax
import jax.numpy as jnp
from jax import lax
from jax.experimental import pallas as pl
from jax.experimental.pallas import tpu as pltpu
from jax.sharding import PartitionSpec as P

norm_epsilon = 1e-05
adapter_scale_factor = 1.0
rope_base = 500000.0
masked_score = -1e30

IN_VMEM = pl.BlockSpec(memory_space=pltpu.VMEM)
IN_PLACE = pl.BlockSpec(memory_space=pltpu.HBM)


def exchanged(parts):
    return lax.all_to_all(parts, "seq", 0, 0, tiled=True)


def iota(shape, axis):
    return lax.broadcasted_iota(jnp.int32, shape, axis)


def rounded(value):
    return value.astype(jnp.bfloat16).astype(jnp.float32)


def started(source, target, sem):
    copy = pltpu.make_async_copy(source, target, sem)
    copy.start()
    return copy


def owned_column(choice_ref, first, count):
    requests = choice_ref.shape[0]
    row = iota((requests, 1), 0)
    column = jnp.zeros((requests, 1), jnp.int32)
    for r in range(requests):
        local = choice_ref[r] - first
        held = ((local >= 0) & (local < count)).astype(jnp.int32)
        column = jnp.where(row == r, held, column)
    return column > 0


def small_sums_kernel(
    choice_hbm,
    hidden_hbm,
    gain_hbm,
    down_ref,
    message_ref,
    scaled_ref,
    choice_ref,
    hidden_ref,
    gain_ref,
    rows_ref,
    sems,
):
    requests, rank, width = rows_ref.shape
    count = down_ref.shape[0]
    head_index = lax.axis_index("head")
    first = head_index * count
    choice_copy = started(choice_hbm, choice_ref, sems.at[requests])
    hidden_copy = started(hidden_hbm, hidden_ref, sems.at[requests + 1])
    gain_copy = started(gain_hbm, gain_ref, sems.at[requests + 2])
    choice_copy.wait()
    copies = []
    for r in range(requests):
        local = jnp.clip(choice_ref[r] - first, 0, count - 1)
        copies.append(started(down_ref.at[local], rows_ref.at[r], sems.at[r]))
    hidden_copy.wait()
    gain_copy.wait()
    values = hidden_ref[...].astype(jnp.float32)
    gain = gain_ref[...].astype(jnp.float32).reshape(1, width)
    scaled = (values * gain).astype(jnp.bfloat16)
    scaled_ref[...] = scaled
    squares = jnp.sum(values * values, axis=1, keepdims=True)
    squares = jnp.where(head_index == 0, squares, 0.0)
    diagonal = iota((requests, 128), 1) == iota((requests, 128), 0)
    squares = jnp.sum(jnp.where(diagonal, squares, 0.0), axis=0, keepdims=True)
    owned = owned_column(choice_ref, first, count)
    for copy in copies:
        copy.wait()
    products = lax.dot_general(
        scaled,
        rows_ref[...].reshape(requests * rank, width),
        (((1,), (1,)), ((), ())),
        preferred_element_type=jnp.float32,
    )
    keep = (iota(products.shape, 1) // rank == iota(products.shape, 0)) & owned
    sums = jnp.sum(jnp.where(keep, products, 0.0), axis=0, keepdims=True)
    message = jnp.concatenate([sums, squares], axis=1)
    message_ref[...] = jnp.broadcast_to(message[None], message_ref.shape)


def projection_kernel(
    own_rows,
    choice_hbm,
    lengths_hbm,
    scaled_ref,
    query_ref,
    key_ref,
    value_ref,
    up_ref,
    part_ref,
    up_rows_ref,
    owned_ref,
    table_ref,
    choice_ref,
    lengths_ref,
    query_buf,
    key_buf,
    value_buf,
    sems,
):
    requests = scaled_ref.shape[0]
    head_dim = table_ref.shape[1]
    columns, kv_columns = query_ref.shape[1], key_ref.shape[1]
    count = up_ref.shape[0]
    first = lax.axis_index("seq") * count
    chunk = min(columns, 1024)
    pieces = []
    for start in range(0, columns, chunk):
        window = (slice(None), pl.ds(start, chunk))
        pieces.append((query_ref.at[window], query_buf.at[window], start, chunk))
    pieces.append((key_ref, key_buf, columns, kv_columns))
    pieces.append((value_ref, value_buf, columns + kv_columns, kv_columns))
    others = len(pieces) + requests

    def up_copy(r, local):
        return pltpu.make_async_copy(
            up_ref.at[local], up_rows_ref.at[r], sems.at[len(pieces) + r]
        )

    choice_copy = started(choice_hbm, choice_ref, sems.at[others])
    lengths_copy = started(lengths_hbm, lengths_ref, sems.at[others + 1])
    copies = [
        started(source, target, sems.at[k]) for k, (source, target, _, _) in enumerate(pieces)
    ]
    choice_copy.wait()
    for r in range(requests):
        local = choice_ref[r] - first
        held = (local >= 0) & (local < count)

        @pl.when(held)
        def _(r=r, local=local):
            up_copy(r, local).start()

        @pl.when(jnp.logical_not(held))
        def _(r=r):
            up_rows_ref[r] = jnp.zeros(up_rows_ref.shape[1:], up_rows_ref.dtype)

    owned_ref[...] = jnp.broadcast_to(
        owned_column(choice_ref, first, count).astype(jnp.float32), owned_ref.shape
    )
    lengths_copy.wait()
    own_request = lax.axis_index("seq") * own_rows // (columns // head_dim)
    position = lengths_ref[own_request].astype(jnp.float32)
    half_dim = head_dim // 2
    lane = iota((1, head_dim), 1)
    step = jnp.where(lane < half_dim, lane, lane - half_dim).astype(jnp.float32)
    angles = position * jnp.exp(-step * (math.log(rope_base) / half_dim))
    sine_val = jnp.sin(angles)
    table_ref[0:1, :] = jnp.cos(angles)
    table_ref[1:2, :] = jnp.where(lane < half_dim, -sine_val, sine_val)
    scaled = scaled_ref[...]
    for copy, (_, target, start, size) in zip(copies, pieces):
        copy.wait()
        part_ref[:, pl.ds(start, size)] = jnp.dot(
            scaled, target[...], preferred_element_type=jnp.float32
        )
    for r in range(requests):
        local = choice_ref[r] - first

        @pl.when((local >= 0) & (local < count))
        def _(r=r, local=local):
            up_copy(r, local).wait()


def query_parts_kernel(
    model_width, owned_ref, small_ref, part_ref, up_rows_ref, message_ref, rows_ref
):
    requests, rank, columns = up_rows_ref.shape
    devices, message_rows, head_dim = message_ref.shape
    heads = columns // head_dim
    all_heads = part_ref.shape[1] // head_dim
    kv_heads = (all_heads - heads) // 2
    own_rows = requests * heads // devices
    own_kv = (message_rows - own_rows) // 2
    small = jnp.sum(small_ref[...], axis=0)
    sums, squares = small[:, : requests * rank], small[:, requests * rank :]
    diagonal = iota((requests, 128), 1) == iota((requests, 128), 0)
    squares = jnp.sum(jnp.where(diagonal, squares, 0.0), axis=1, keepdims=True)
    inverse = lax.rsqrt(squares / model_width + norm_epsilon)
    shape = (requests, requests * rank)
    keep = (iota(shape, 1) // rank == iota(shape, 0)) & (owned_ref[:, 0:1] > 0)
    shrunk = sums * inverse * adapter_scale_factor
    shrunk = jnp.where(keep, shrunk, 0.0).astype(jnp.bfloat16)
    expand = jnp.dot(
        shrunk,
        up_rows_ref[...].reshape(requests * rank, columns),
        preferred_element_type=jnp.float32,
    )
    for h in range(all_heads):
        window = slice(h * head_dim, (h + 1) * head_dim)
        rows = part_ref[:, window] * inverse
        if h < heads:
            rows = rows + expand[:, window]
        rows_ref[pl.ds(h * requests, requests), :] = rows
    for t in range(devices):
        r, h = divmod(t * own_rows, heads)
        kv = h * kv_heads // heads

        def taken(first, count):
            return rows_ref[pl.ds(first * requests + r, count, stride=requests), :]

        if own_rows == heads:
            block = taken(0, all_heads)
        else:
            block = jnp.concatenate(
                [taken(h, own_rows), taken(heads + kv, own_kv), taken(heads + kv_heads + kv, own_kv)]
            )
        message_ref[t] = block.astype(jnp.bfloat16)


def rotation_kernel(own_kv, table_ref, parts_ref, spread_ref, own_ref):
    own_rows, head_dim = spread_ref.shape[1:]
    group = own_rows // own_kv
    sums = jnp.sum(parts_ref[...].astype(jnp.float32), axis=0)
    cosine, sine_val = table_ref[0:1, :], table_ref[1:2, :]
    rotated = rounded(
        sums * cosine + pltpu.roll(sums, head_dim // 2, 1) * sine_val
    )
    query_rot = rotated[:own_rows]
    spread_ref[...] = jnp.broadcast_to(query_rot.astype(jnp.bfloat16)[None], spread_ref.shape)

    def repeated(rows):
        return jnp.concatenate(
            [jnp.broadcast_to(rows[k : k + 1], (group, head_dim)) for k in range(own_kv)]
        )

    key_rot = repeated(rotated[own_rows : own_rows + own_kv])
    own_score = jnp.sum(query_rot * key_rot, axis=1, keepdims=True) * head_dim ** (-0.5)
    own_ref[0] = jnp.broadcast_to(own_score, (own_rows, head_dim))
    own_ref[1] = repeated(rounded(sums[own_rows + own_kv : own_rows + 2 * own_kv]))


def attention_kernel(
    kv_heads,
    lengths_hbm,
    query_ref,
    key_ref,
    value_ref,
    message_ref,
    lengths_ref,
    weights_ref,
    stats_ref,
    sem,
):
    requests, entries, head_dim = key_ref.shape
    cached = entries // kv_heads
    devices, message_rows, _ = message_ref.shape
    heads = query_ref.shape[0] // requests
    own_rows = requests * heads // devices
    group = heads // kv_heads
    lengths_copy = started(lengths_hbm, lengths_ref, sem)
    first = lax.axis_index("seq") * cached
    shape = (heads, entries)
    column = iota(shape, 1)
    same_head = column % kv_heads == iota(shape, 0) // group
    position = jnp.where(same_head, first + column // kv_heads, jnp.int32(2**30))
    lane = iota((heads, head_dim), 1)
    row = iota((heads, head_dim), 0)
    lengths_copy.wait()
    for r in range(requests):
        scores = lax.dot_general(
            query_ref[pl.ds(r * heads, heads), :],
            key_ref[r],
            (((1,), (1,)), ((), ())),
            preferred_element_type=jnp.float32,
        ) * head_dim ** (-0.5)
        valid = position < lengths_ref[r]
        scores = jnp.where(valid, scores, masked_score)
        peak = jnp.max(scores, axis=1, keepdims=True)
        shift_high = rounded(peak)
        shift_low = rounded(peak - shift_high)
        weights = jnp.where(valid, jnp.exp(scores - (shift_high + shift_low)), 0.0)
        total = jnp.sum(weights, axis=1, keepdims=True)
        total_high = rounded(total)
        total_low = rounded(total - total_high)
        weights_ref[r] = weights.astype(jnp.bfloat16)
        stats = jnp.zeros((heads, head_dim), jnp.float32)
        for k, piece in enumerate((shift_high, shift_low, total_high, total_low)):
            stats = jnp.where(lane == k * own_rows + row % own_rows, piece, stats)
        stats_ref[r] = stats
    for r in range(requests):
        out = jnp.dot(weights_ref[r], value_ref[r], preferred_element_type=jnp.float32)
        for part in range(heads // own_rows):
            window = slice(part * own_rows, (part + 1) * own_rows)
            stats_row = jnp.sum(stats_ref[r, window, :], axis=0, keepdims=True)
            filler = jnp.broadcast_to(stats_row, (message_rows - own_rows, head_dim))
            block = jnp.concatenate([out[window], filler])
            message_ref[r * (heads // own_rows) + part] = block.astype(jnp.bfloat16)


def combine_kernel(parts_ref, own_ref, spread_ref):
    devices, own_rows, head_dim = spread_ref.shape
    lane = iota((own_rows, head_dim), 1)
    row = iota((own_rows, head_dim), 0)
    own_score = own_ref[0][:, 0:1]
    shifts, totals = [], []
    overall = own_score
    for s in range(devices):
        stats = parts_ref[s].astype(jnp.float32)[own_rows : own_rows + 1]
        shift = jnp.sum(
            jnp.where((lane == row) | (lane == own_rows + row), stats, 0.0), axis=1, keepdims=True
        )
        total = jnp.sum(
            jnp.where((lane == 2 * own_rows + row) | (lane == 3 * own_rows + row), stats, 0.0),
            axis=1,
            keepdims=True,
        )
        shifts.append(shift)
        totals.append(total)
        overall = jnp.maximum(overall, shift)
    own_weight = jnp.exp(own_score - overall)
    denominator = own_weight
    summed = own_weight * own_ref[1]
    for s in range(devices):
        factor = jnp.exp(shifts[s] - overall)
        denominator = denominator + totals[s] * factor
        summed = summed + factor * parts_ref[s].astype(jnp.float32)[:own_rows]
    attended = (summed / denominator).astype(jnp.bfloat16)
    spread_ref[...] = jnp.broadcast_to(attended[None], spread_ref.shape)


def output_kernel(attended_ref, weight_ref, out_ref, rows_ref):
    requests = out_ref.shape[0]
    heads = attended_ref.shape[0] // requests
    rows_ref[...] = attended_ref[...].astype(jnp.float32)
    left = jnp.concatenate(
        [rows_ref[pl.ds(h, requests, stride=heads), :] for h in range(heads)], axis=1
    ).astype(jnp.bfloat16)
    out_ref[...] = jnp.dot(left, weight_ref[...], preferred_element_type=jnp.float32)


def called(kernel, out_shape, in_specs, scratch=(), flops=0, read=0):
    call = pl.pallas_call(
        kernel,
        out_shape=out_shape,
        in_specs=in_specs,
        out_specs=jax.tree.map(lambda _: IN_VMEM, out_shape),
        scratch_shapes=list(scratch),
        cost_estimate=pl.CostEstimate(flops=flops, transcendentals=0, bytes_accessed=read),
        compiler_params=pltpu.CompilerParams(vmem_limit_bytes=28 << 20),
    )

    def run(*operands):
        return call(
            *(
                pltpu.with_memory_space_constraint(operand, pltpu.HBM)
                if spec is IN_PLACE
                else operand
                for operand, spec in zip(operands, in_specs, strict=True)
            )
        )

    return run


def body(
    hidden_state_input,
    attention_norm_gain,
    query_projection_matrix,
    key_projection_matrix,
    value_projection_matrix,
    output_projection_matrix,
    adapter_down_matrix,
    adapter_up_matrix,
    adapter_choice_index,
    lengths,
    rotated_key_cache,
    cached_value_rows,
):
    f32, bf16 = jnp.float32, jnp.bfloat16
    requests, width = hidden_state_input.shape
    _, cached, kv_heads, head_dim = rotated_key_cache.shape
    columns = query_projection_matrix.shape[1]
    kv_columns = key_projection_matrix.shape[1]
    heads = columns // head_dim
    rank = adapter_down_matrix.shape[1]
    devices = lax.axis_size("seq")
    head_size = lax.axis_size("head")
    everyone = devices * head_size
    group = heads // kv_heads
    own_rows = requests * heads // devices
    own_kv = max(own_rows // group, 1)
    parts_rows = own_rows + 2 * own_kv
    message_rows = (own_rows + 8) // 8 * 8
    sds = jax.ShapeDtypeStruct
    dma = pltpu.SemaphoreType.DMA

    small, scaled = called(
        small_sums_kernel,
        (sds((everyone, 1, requests * rank + 128), f32), sds((requests, width), bf16)),
        [IN_PLACE] * 4,
        [
            pltpu.SMEM((requests,), jnp.int32),
            pltpu.VMEM((requests, width), bf16),
            pltpu.VMEM((width,), bf16),
            pltpu.VMEM((requests, rank, width), bf16),
            dma((requests + 3,)),
        ],
    )(adapter_choice_index, hidden_state_input, attention_norm_gain, adapter_down_matrix)
    small = lax.all_to_all(small, ("seq", "head"), 0, 0, tiled=True)
    pieces = -(-columns // 1024) + 2
    part, up_rows, owned, table = called(
        functools.partial(projection_kernel, own_rows),
        (
            sds((requests, columns + 2 * kv_columns), f32),
            sds((requests, rank, columns), bf16),
            sds((requests, 128), f32),
            sds((2, head_dim), f32),
        ),
        [IN_PLACE, IN_PLACE, IN_VMEM, IN_PLACE, IN_PLACE, IN_PLACE, IN_PLACE],
        [
            pltpu.SMEM((requests,), jnp.int32),
            pltpu.SMEM((requests,), jnp.int32),
            pltpu.VMEM((width, columns), bf16),
            pltpu.VMEM((width, kv_columns), bf16),
            pltpu.VMEM((width, kv_columns), bf16),
            dma((pieces + requests + 2,)),
        ],
        flops=2 * requests * width * (columns + 2 * kv_columns),
        read=2 * width * (columns + 2 * kv_columns),
    )(
        adapter_choice_index,
        lengths,
        scaled,
        query_projection_matrix,
        key_projection_matrix,
        value_projection_matrix,
        adapter_up_matrix,
    )
    parts = called(
        functools.partial(query_parts_kernel, width * devices),
        sds((devices, parts_rows, head_dim), bf16),
        [IN_VMEM] * 4,
        [pltpu.VMEM(((heads + 2 * kv_heads) * requests, head_dim), f32)],
        flops=16 << 30,
        read=16 << 20,
    )(owned, small, part, up_rows)
    parts = exchanged(parts)

    spread, own = called(
        functools.partial(rotation_kernel, own_kv),
        (sds((devices, own_rows, head_dim), bf16), sds((2, own_rows, head_dim), f32)),
        [IN_VMEM, IN_VMEM],
        flops=16 << 30,
        read=16 << 20,
    )(table, parts)
    query_rot = exchanged(spread).reshape(requests * heads, head_dim)

    entries = cached * kv_heads
    parts = called(
        functools.partial(attention_kernel, kv_heads),
        sds((devices, message_rows, head_dim), bf16),
        [IN_PLACE, IN_VMEM, IN_VMEM, IN_VMEM],
        [
            pltpu.SMEM((requests,), jnp.int32),
            pltpu.VMEM((requests, heads, entries), bf16),
            pltpu.VMEM((requests, heads, head_dim), f32),
            dma(()),
        ],
        flops=4 * requests * heads * entries * head_dim,
        read=16 << 20,
    )(
        lengths,
        query_rot,
        rotated_key_cache.reshape(requests, entries, head_dim),
        cached_value_rows.reshape(requests, entries, head_dim),
    )
    parts = exchanged(parts)
    spread = called(
        combine_kernel, sds((devices, own_rows, head_dim), bf16), [IN_VMEM, IN_VMEM]
    )(parts, own)
    attended = exchanged(spread).reshape(requests * heads, head_dim)
    out_columns = output_projection_matrix.shape[1]
    out_part = called(
        output_kernel,
        sds((requests, out_columns), f32),
        [IN_VMEM, IN_VMEM],
        [pltpu.VMEM((requests * heads, head_dim), f32)],
    )(attended, output_projection_matrix)
    if head_size == 2:
        output_sum = out_part + lax.ppermute(out_part, "head", [(0, 1), (1, 0)])
    else:
        output_sum = lax.psum(out_part, "head")
    return output_sum.astype(jnp.bfloat16)


def solution(mesh):
    return jax.shard_map(
        body,
        mesh=mesh,
        in_specs=(
            P(None, "seq"),
            P("seq"),
            P("seq", "head"),
            P("seq", "head"),
            P("seq", "head"),
            P("head", "seq"),
            P("head", None, "seq"),
            P("seq", None, "head"),
            P(),
            P(),
            P(None, "seq", "head", None),
            P(None, "seq", "head", None),
        ),
        out_specs=P(None, "seq"),
        check_vma=False,
    )
```

time: 360 us -> 68.1 us (0.19)
  waiting for transfers between devices: 169 us -> 5.51 us
  blocking collectives: 125 us -> 43.4 us
  other arithmetic: 27.1 us -> 0.61 us
  matrix products: 15.6 us -> 0 us
  between operations: 13.3 us -> 0.06 us
  Pallas kernels: 0 us -> 10.7 us
  local copies, waits for them, and re-layouts: 8.98 us -> 0.01 us
  starting transfers between devices: 0.09 us -> 7.33 us
    psum x2 -> x0, waiting for transfers between devices: 168 us -> none  [the longest x1 112 us: body(): up_sum = lax.psum(expand, 'seq')]
    all_gather x2 -> x0, blocking collectives: 79.1 us -> none  [joined(): lax.all_gather(part.astype(kind), axis)]
    psum x2 -> x0, blocking collectives: 46 us -> none  [the longest x1 42 us: body(): down_total_sum = lax.psum(down_part, ('seq', 'head'))]
    all_to_all x0 -> x4, blocking collectives: none -> 43.4 us  [exchanged(): return lax.all_to_all(parts, 'seq', 0, 0, tiled=True)]
    add x32 -> x0, other arithmetic: 18 us -> none  [the longest x15 17.6 us: combine_parts(): out_one * scale_one[..., None] + out_two * scale_two[..., None]]
    dot_general x9 -> x0, matrix products: 15.6 us -> none  [the longest x1 3.56 us: body(): jnp.dot(scaled, query_projection_matrix, preferred_element_type=jnp.float32)]
    pallas_call x0 -> x7, Pallas kernels: none -> 10.7 us  [run(): call(*(pltpu.with_memory_space_constraint(operand, pltpu.HBM) if spec is...]
    all_to_all x0 -> x1, starting transfers between devices: none -> 7.33 us  [body(): small = lax.all_to_all(small, ('seq', 'head'), 0, 0, tiled=True)]
  transfers between devices with their start and end apart: 3 -> 2, of which waited for: 2 -> 2; matrix products, arithmetic and copies ran while one was open for 4% -> 0% of each run, Pallas kernels for 0% -> 4%
where the time goes in v2:
time: 68.1 us; the launch traced here: 67.7 us
  blocking collectives  43.4 us (64%)
  Pallas kernels  10.7 us (16%)
  starting transfers between devices  7.33 us (11%)
  waiting for transfers between devices  5.51 us (8%)
    all_to_all x4, blocking collectives, exchanged(): return lax.all_to_all(parts, 'seq', 0, 0, tiled=True)  43.4 us
    pallas_call x7, Pallas kernels, run(): call(*(pltpu.with_memory_space_constraint(operand, pltpu.HBM) if spec is...  10.7 us
    all_to_all x1, starting transfers between devices, body(): small = lax.all_to_all(small, ('seq', 'head'), 0, 0, tiled=True)  7.33 us
    all_to_all x1, waiting for transfers between devices, body(): small = lax.all_to_all(small, ('seq', 'head'), 0, 0, tiled=True)  4.29 us
  transfers between devices with their start and end apart: 2, of which 2 were waited for; matrix products, arithmetic and copies ran while one was open for 0% of the time, Pallas kernels for 4%

profile of v2, /device:TPU:0, one launch (start us, length us, event | category | flops | bytes accessed | tf_op | source)
XLA Modules:
  0.0 67.7 jit_solution(12963465437860621959)
XLA Ops:
  0.0 2.7 %shard_map.118 = (f32[32,1,384]{2,1,0:T(1,128)}, bf16[16,512]{1,0:T(8,128)(2,1)S(1)}) custom-call(s32[16]{0:T(128)} %choice_hbm.3, bf16[16,512]{1,0:T(8,128)(2,1)} %hidden_hbm.1, bf16[512]{0:T(512)(128)(2,1)} %gain_hbm.1, bf16[256,16,512]{2,1,0:T(8,128)(2,1)} %down_ref.1), custom_call_target="tpu_custom_call" | custom-call | tf_op jit(solution)/shard_map/pallas_call | solution.py:362
  2.7 7.3 %all-to-all-start = ((f32[32,1,384]{2,1,0:T(1,128)}), f32[32,1,384]{2,1,0:T(1,128)S(1)}, u32[]{:S(2)}, u32[]{:S(2)}) async-start(f32[32,1,384]{2,1,0:T(1,128)} %get-tuple-element.16), calls=%async_computation | async-start | bytes 98304 | tf_op jit(solution)/shard_map/all_to_all | solution.py:418
  10.0 3.0 %shard_map.119 = (f32[16,5120]{1,0:T(8,128)S(1)}, bf16[16,16,4096]{2,1,0:T(8,128)(2,1)S(1)}, f32[16,128]{1,0:T(8,128)S(1)}, f32[2,128]{1,0:T(2,128)S(1)}) custom-call(s32[16]{0:T(128)} %choice_hbm.3, s32[16]{0:T(128)} %lengths_hbm.3, bf16[16,512]{1,0:T(8,128)(2,1)S(1)} %get-tuple-element.13.scaled_ref, bf16[512,4096]{1,0:T(8,128)(2,1)} %query_ref.1, ...), custom_call_target="tpu_custom_call" | custom-call | flops 83886080 | bytes 5242880 | tf_op jit(solution)/shard_map/pallas_call | solution.py:362
  13.1 4.3 %all-to-all-done.small_ref = f32[32,1,384]{2,1,0:T(1,128)S(1)} async-done(((f32[32,1,384]{2,1,0:T(1,128)}), f32[32,1,384]{2,1,0:T(1,128)S(1)}, u32[]{:S(2)}, u32[]{:S(2)}) %all-to-all-start) | async-done | bytes 49184 | tf_op jit(solution)/shard_map/all_to_all | solution.py:418
  17.4 0.5 shard_map.120
  17.9 11.0 %all_to_all.25.parts_ref = bf16[16,40,128]{2,1,0:T(8,128)(2,1)S(1)} all-to-all(bf16[16,40,128]{2,1,0:T(8,128)(2,1)S(1)} %shard_map.120), channel_id=1, replica_groups=mesh['seq'=16,'head'=2] {'seq'}, dimensions={0} | all-to-all | bytes 327680 | tf_op jit(solution)/shard_map/all_to_all | solution.py:21
  28.9 0.0 copy-start
  28.9 0.0 copy-start.1
  28.9 0.2 shard_map.121
  29.0 11.3 %all_to_all.26 = bf16[16,32,128]{2,1,0:T(8,128)(2,1)S(1)} all-to-all(bf16[16,32,128]{2,1,0:T(8,128)(2,1)S(1)} %get-tuple-element.19), channel_id=1, replica_groups=mesh['seq'=16,'head'=2] {'seq'}, dimensions={0} | all-to-all | bytes 262144 | tf_op jit(solution)/shard_map/all_to_all | solution.py:21
  40.3 0.0 copy-done
  40.3 0.0 copy-done.1
  40.3 0.0 copy-start.2
  40.3 3.3 %shard_map.122 = bf16[16,40,128]{2,1,0:T(8,128)(2,1)S(1)} custom-call(s32[16]{0:T(128)} %lengths_hbm.3, bf16[512,128]{1,0:T(8,128)(2,1)S(1)} %bitcast.6, bf16[16,1024,128]{2,1,0:T(8,128)(2,1)S(1)} %bitcast.4, bf16[16,1024,128]{2,1,0:T(8,128)(2,1)S(1)} %bitcast.5), custom_call_target="tpu_custom_call" | custom-call | flops 268435456 | bytes 16777216 | tf_op jit(solution)/shard_map/pallas_call | solution.py:362
  43.6 10.5 %all_to_all.27.parts_ref = bf16[16,40,128]{2,1,0:T(8,128)(2,1)S(1)} all-to-all(bf16[16,40,128]{2,1,0:T(8,128)(2,1)S(1)} %shard_map.122), channel_id=1, replica_groups=mesh['seq'=16,'head'=2] {'seq'}, dimensions={0} | all-to-all | bytes 327680 | tf_op jit(solution)/shard_map/all_to_all | solution.py:21
  54.1 0.4 shard_map.123
  54.5 10.6 %all_to_all.28 = bf16[16,32,128]{2,1,0:T(8,128)(2,1)S(1)} all-to-all(bf16[16,32,128]{2,1,0:T(8,128)(2,1)S(1)} %shard_map.123), channel_id=1, replica_groups=mesh['seq'=16,'head'=2] {'seq'}, dimensions={0} | all-to-all | bytes 262144 | tf_op jit(solution)/shard_map/all_to_all | solution.py:21
  65.2 0.0 copy-done.2
  65.2 0.7 shard_map.124
  65.8 0.0 collective-permute-start
  65.8 1.2 %collective-permute-done = f32[16,512]{1,0:T(8,128)S(1)} collective-permute-done((f32[16,512]{1,0:T(8,128)S(1)}, f32[16,512]{1,0:T(8,128)S(1)}, u32[]{:S(2)}, u32[]{:S(2)}) %collective-permute-start) | collective-permute-done | bytes 32800 | tf_op jit(solution)/shard_map/ppermute | solution.py:499
  67.0 0.6 add_convert_fusion
Async XLA Ops:
  2.7 14.7 %all-to-all-start = ((f32[32,1,384]{2,1,0:T(1,128)}), f32[32,1,384]{2,1,0:T(1,128)S(1)}, u32[]{:S(2)}, u32[]{:S(2)}) async-start(f32[32,1,384]{2,1,0:T(1,128)} %get-tuple-element.16), calls=%async_computation | async-start | bytes 98304 | tf_op jit(solution)/shard_map/all_to_all | solution.py:418
  28.9 11.4 %copy-start = (bf16[16,256,4,128]{3,2,1,0:T(4,128)(2,1)S(1)}, bf16[16,256,4,128]{3,2,1,0:T(4,128)(2,1)}, u32[]{:S(2)}) copy-start(bf16[16,256,4,128]{3,2,1,0:T(4,128)(2,1)} %param.22) | copy-start | bytes 12582916
  28.9 11.4 %copy-start.1 = (bf16[16,256,4,128]{3,2,1,0:T(4,128)(2,1)S(1)}, bf16[16,256,4,128]{3,2,1,0:T(4,128)(2,1)}, u32[]{:S(2)}) copy-start(bf16[16,256,4,128]{3,2,1,0:T(4,128)(2,1)} %param.23) | copy-start | bytes 12582916
  40.3 24.9 %copy-start.2 = (bf16[4096,512]{1,0:T(8,128)(2,1)S(1)}, bf16[4096,512]{1,0:T(8,128)(2,1)}, u32[]{:S(2)}) copy-start(bf16[4096,512]{1,0:T(8,128)(2,1)} %weight_ref.1) | copy-start | bytes 12582916
  65.8 1.2 %collective-permute-start = (f32[16,512]{1,0:T(8,128)S(1)}, f32[16,512]{1,0:T(8,128)S(1)}, u32[]{:S(2)}, u32[]{:S(2)}) collective-permute-start(f32[16,512]{1,0:T(8,128)S(1)} %shard_map.124), channel_id=1, source_target_pairs={{0,1},{1,0},{2,3},{3,2},{4,5},{5,4},{6,7},{7,6},{8,9},{9,8},{10,11... | collective-permute-start | bytes 98312 | tf_op jit(solution)/shard_map/ppermute | solution.py:499

commit v3 on v2

v3 whole, which is shorter than its diff:
```python
import functools
import math

import jax
import jax.numpy as jnp
from jax import lax
from jax.experimental import pallas as pl
from jax.experimental.pallas import tpu as pltpu
from jax.sharding import PartitionSpec as P

norm_epsilon = 1e-05
adapter_scale_factor = 1.0
rope_base = 500000.0
masked_score = -1e30

IN_VMEM = pl.BlockSpec(memory_space=pltpu.VMEM)
IN_PLACE = pl.BlockSpec(memory_space=pltpu.HBM)


def exchanged(parts):
    return lax.all_to_all(parts, "seq", 0, 0, tiled=True)


def iota(shape, axis):
    return lax.broadcasted_iota(jnp.int32, shape, axis)


def rounded(value):
    return value.astype(jnp.bfloat16).astype(jnp.float32)


def started(source, target, sem):
    copy = pltpu.make_async_copy(source, target, sem)
    copy.start()
    return copy


def owned_column(choice_ref, first, count):
    requests = choice_ref.shape[0]
    row = iota((requests, 1), 0)
    column = jnp.zeros((requests, 1), jnp.int32)
    for r in range(requests):
        local = choice_ref[r] - first
        held = ((local >= 0) & (local < count)).astype(jnp.int32)
        column = jnp.where(row == r, held, column)
    return column > 0


def small_sums_kernel(
    own_rows,
    choice_hbm,
    lengths_hbm,
    hidden_hbm,
    gain_hbm,
    down_ref,
    up_ref,
    message_ref,
    scaled_ref,
    up_rows_ref,
    owned_ref,
    table_ref,
    limits_ref,
    choice_ref,
    lengths_ref,
    hidden_ref,
    gain_ref,
    down_rows_ref,
    sems,
    down_sems,
    up_sems,
):
    requests, rank, width = down_rows_ref.shape
    columns, head_dim = up_ref.shape[2], table_ref.shape[1]
    choice_copy = started(choice_hbm, choice_ref, sems.at[0])
    lengths_copy = started(lengths_hbm, lengths_ref, sems.at[1])
    hidden_copy = started(hidden_hbm, hidden_ref, sems.at[2])
    gain_copy = started(gain_hbm, gain_ref, sems.at[3])
    head_index = lax.axis_index("head")
    down_count, up_count = down_ref.shape[0], up_ref.shape[0]
    down_first = head_index * down_count
    up_first = lax.axis_index("seq") * up_count

    def up_copy(r):
        local = choice_ref[r] - up_first
        return pltpu.make_async_copy(up_ref.at[local], up_rows_ref.at[r], up_sems.at[r])

    def up_held(r):
        local = choice_ref[r] - up_first
        return (local >= 0) & (local < up_count)

    choice_copy.wait()
    down_copies = []
    for r in range(requests):
        local = jnp.clip(choice_ref[r] - down_first, 0, down_count - 1)
        down_copies.append(started(down_ref.at[local], down_rows_ref.at[r], down_sems.at[r]))
    for r in range(requests):

        @pl.when(up_held(r))
        def _(r=r):
            up_copy(r).start()

        @pl.when(jnp.logical_not(up_held(r)))
        def _(r=r):
            up_rows_ref[r] = jnp.zeros(up_rows_ref.shape[1:], up_rows_ref.dtype)

    owned_ref[...] = jnp.broadcast_to(
        owned_column(choice_ref, up_first, up_count).astype(jnp.float32), owned_ref.shape
    )
    lengths_copy.wait()
    for r in range(requests):
        limits_ref[pl.ds(r, 1), :] = jnp.full((1, limits_ref.shape[1]), lengths_ref[r], jnp.int32)
    own_request = lax.axis_index("seq") * own_rows // (columns // head_dim)
    position = lengths_ref[own_request].astype(jnp.float32)
    half_dim = head_dim // 2
    lane = iota((1, head_dim), 1)
    step = jnp.where(lane < half_dim, lane, lane - half_dim).astype(jnp.float32)
    angles = position * jnp.exp(-step * (math.log(rope_base) / half_dim))
    sine_val = jnp.sin(angles)
    table_ref[0:1, :] = jnp.cos(angles)
    table_ref[1:2, :] = jnp.where(lane < half_dim, -sine_val, sine_val)

    hidden_copy.wait()
    gain_copy.wait()
    values = hidden_ref[...].astype(jnp.float32)
    gain = gain_ref[...].astype(jnp.float32).reshape(1, width)
    scaled = (values * gain).astype(jnp.bfloat16)
    scaled_ref[...] = scaled
    squares = jnp.sum(values * values, axis=1, keepdims=True)
    squares = jnp.where(head_index == 0, squares, 0.0)
    diagonal = iota((requests, 128), 1) == iota((requests, 128), 0)
    squares = jnp.sum(jnp.where(diagonal, squares, 0.0), axis=0, keepdims=True)
    owned = owned_column(choice_ref, down_first, down_count)
    for copy in down_copies:
        copy.wait()
    products = lax.dot_general(
        scaled,
        down_rows_ref[...].reshape(requests * rank, width),
        (((1,), (1,)), ((), ())),
        preferred_element_type=jnp.float32,
    )
    keep = (iota(products.shape, 1) // rank == iota(products.shape, 0)) & owned
    sums = jnp.sum(jnp.where(keep, products, 0.0), axis=0, keepdims=True)
    message = jnp.concatenate([sums, squares], axis=1)
    message_ref[...] = jnp.broadcast_to(message[None], message_ref.shape)
    for r in range(requests):

        @pl.when(up_held(r))
        def _(r=r):
            up_copy(r).wait()


def query_parts_kernel(
    model_width,
    owned_ref,
    small_ref,
    scaled_ref,
    query_ref,
    key_ref,
    value_ref,
    up_rows_ref,
    message_ref,
    rows_ref,
):
    requests, rank, columns = up_rows_ref.shape
    devices, message_rows, head_dim = message_ref.shape
    heads = columns // head_dim
    kv_heads = key_ref.shape[1] // head_dim
    all_heads = heads + 2 * kv_heads
    own_rows = requests * heads // devices
    own_kv = (message_rows - own_rows) // 2
    small = jnp.sum(small_ref[...], axis=0)
    sums, squares = small[:, : requests * rank], small[:, requests * rank :]
    diagonal = iota((requests, 128), 1) == iota((requests, 128), 0)
    squares = jnp.sum(jnp.where(diagonal, squares, 0.0), axis=1, keepdims=True)
    inverse = lax.rsqrt(squares / model_width + norm_epsilon)
    shape = (requests, requests * rank)
    keep = (iota(shape, 1) // rank == iota(shape, 0)) & (owned_ref[:, 0:1] > 0)
    shrunk = sums * inverse * adapter_scale_factor
    shrunk = jnp.where(keep, shrunk, 0.0).astype(jnp.bfloat16)
    scaled = scaled_ref[...]
    up_rows = up_rows_ref.reshape(requests * rank, columns)
    chunk = min(columns, 1024)
    first_head = 0
    for weight_ref in (query_ref, key_ref, value_ref):
        for start in range(0, weight_ref.shape[1], chunk):
            size = min(chunk, weight_ref.shape[1] - start)
            part = jnp.dot(
                scaled, weight_ref[:, pl.ds(start, size)], preferred_element_type=jnp.float32
            )
            part = part * inverse
            if weight_ref is query_ref:
                part = part + jnp.dot(
                    shrunk, up_rows[:, pl.ds(start, size)], preferred_element_type=jnp.float32
                )
            for k in range(size // head_dim):
                h = first_head + start // head_dim + k
                rows_ref[pl.ds(h * requests, requests), :] = part[
                    :, k * head_dim : (k + 1) * head_dim
                ]
        first_head += weight_ref.shape[1] // head_dim
    for t in range(devices):
        r, h = divmod(t * own_rows, heads)
        kv = h * kv_heads // heads

        def taken(first, count):
            return rows_ref[pl.ds(first * requests + r, count, stride=requests), :]

        if own_rows == heads:
            block = taken(0, all_heads)
        else:
            block = jnp.concatenate(
                [taken(h, own_rows), taken(heads + kv, own_kv), taken(heads + kv_heads + kv, own_kv)]
            )
        message_ref[t] = block.astype(jnp.bfloat16)


def rotation_kernel(own_kv, table_ref, parts_ref, spread_ref, own_ref):
    own_rows, head_dim = spread_ref.shape[1:]
    group = own_rows // own_kv
    sums = jnp.sum(parts_ref[...].astype(jnp.float32), axis=0)
    cosine, sine_val = table_ref[0:1, :], table_ref[1:2, :]
    rotated = rounded(
        sums * cosine + pltpu.roll(sums, head_dim // 2, 1) * sine_val
    )
    query_rot = rotated[:own_rows]
    spread_ref[...] = jnp.broadcast_to(query_rot.astype(jnp.bfloat16)[None], spread_ref.shape)

    def repeated(rows):
        return jnp.concatenate(
            [jnp.broadcast_to(rows[k : k + 1], (group, head_dim)) for k in range(own_kv)]
        )

    key_rot = repeated(rotated[own_rows : own_rows + own_kv])
    own_score = jnp.sum(query_rot * key_rot, axis=1, keepdims=True) * head_dim ** (-0.5)
    own_ref[0] = jnp.broadcast_to(own_score, (own_rows, head_dim))
    own_ref[1] = repeated(rounded(sums[own_rows + own_kv : own_rows + 2 * own_kv]))


def attention_kernel(
    kv_heads,
    limits_ref,
    query_ref,
    key_ref,
    value_ref,
    message_ref,
    weights_ref,
    stats_ref,
):
    requests, entries, head_dim = key_ref.shape
    cached = entries // kv_heads
    devices, message_rows, _ = message_ref.shape
    heads = query_ref.shape[0] // requests
    own_rows = requests * heads // devices
    group = heads // kv_heads
    first = lax.axis_index("seq") * cached
    shape = (heads, entries)
    column = iota(shape, 1)
    same_head = column % kv_heads == iota(shape, 0) // group
    position = jnp.where(same_head, first + column // kv_heads, jnp.int32(2**30))
    lane = iota((heads, head_dim), 1)
    row = iota((heads, head_dim), 0)
    for r in range(requests):
        scores = lax.dot_general(
            query_ref[pl.ds(r * heads, heads), :],
            key_ref[r],
            (((1,), (1,)), ((), ())),
            preferred_element_type=jnp.float32,
        ) * head_dim ** (-0.5)
        valid = position < limits_ref[pl.ds(r, 1), 0:1]
        scores = jnp.where(valid, scores, masked_score)
        peak = jnp.max(scores, axis=1, keepdims=True)
        peak_high = rounded(peak)
        peak_mid = rounded(peak - peak_high)
        peak_low = peak - peak_high - peak_mid
        weights = jnp.where(valid, jnp.exp(scores - peak), 0.0)
        total = jnp.sum(weights, axis=1, keepdims=True)
        total_high = rounded(total)
        total_low = rounded(total - total_high)
        weights_ref[r] = weights.astype(jnp.bfloat16)
        stats = jnp.zeros((heads, head_dim), jnp.float32)
        for k, piece in enumerate((peak_high, peak_mid, peak_low, total_high)):
            stats = jnp.where(lane == k * own_rows + row % own_rows, piece, stats)
        stats_ref[r, 0] = stats
        stats_ref[r, 1] = jnp.where(lane == row % own_rows, total_low, 0.0)
    for r in range(requests):
        out = jnp.dot(weights_ref[r], value_ref[r], preferred_element_type=jnp.float32)
        for part in range(heads // own_rows):
            window = slice(part * own_rows, (part + 1) * own_rows)
            first_row = jnp.sum(stats_ref[r, 0, window, :], axis=0, keepdims=True)
            second_row = jnp.sum(stats_ref[r, 1, window, :], axis=0, keepdims=True)
            filler_shape = (message_rows - own_rows, head_dim)
            filler = jnp.where(iota(filler_shape, 0) == 0, first_row, second_row)
            block = jnp.concatenate([out[window], filler])
            message_ref[r * (heads // own_rows) + part] = block.astype(jnp.bfloat16)


def combine_kernel(parts_ref, own_ref, spread_ref):
    devices, own_rows, head_dim = spread_ref.shape
    lane = iota((own_rows, head_dim), 1)
    row = iota((own_rows, head_dim), 0)
    own_score = own_ref[0][:, 0:1]
    peaks, totals = [], []
    overall = own_score
    for s in range(devices):
        stats = parts_ref[s].astype(jnp.float32)
        first_row, second_row = stats[own_rows : own_rows + 1], stats[own_rows + 1 : own_rows + 2]
        peak = jnp.where((lane < 3 * own_rows) & (lane % own_rows == row), first_row, 0.0)
        total = jnp.where(lane == 3 * own_rows + row, first_row, 0.0)
        total = total + jnp.where(lane == row, second_row, 0.0)
        peaks.append(jnp.sum(peak, axis=1, keepdims=True))
        totals.append(jnp.sum(total, axis=1, keepdims=True))
        overall = jnp.maximum(overall, peaks[-1])
    own_weight = jnp.exp(own_score - overall)
    denominator = own_weight
    summed = own_weight * own_ref[1]
    for s in range(devices):
        factor = jnp.exp(peaks[s] - overall)
        denominator = denominator + totals[s] * factor
        summed = summed + factor * parts_ref[s].astype(jnp.float32)[:own_rows]
    attended = (summed / denominator).astype(jnp.bfloat16)
    spread_ref[...] = jnp.broadcast_to(attended[None], spread_ref.shape)


def output_kernel(attended_ref, weight_ref, out_ref, rows_ref):
    requests = out_ref.shape[0]
    heads = attended_ref.shape[0] // requests
    rows_ref[...] = attended_ref[...].astype(jnp.float32)
    left = jnp.concatenate(
        [rows_ref[pl.ds(h, requests, stride=heads), :] for h in range(heads)], axis=1
    ).astype(jnp.bfloat16)
    out_ref[...] = jnp.dot(left, weight_ref[...], preferred_element_type=jnp.float32)


def called(kernel, out_shape, in_specs, scratch=(), flops=0, read=0):
    call = pl.pallas_call(
        kernel,
        out_shape=out_shape,
        in_specs=in_specs,
        out_specs=jax.tree.map(lambda _: IN_VMEM, out_shape),
        scratch_shapes=list(scratch),
        cost_estimate=pl.CostEstimate(flops=flops, transcendentals=0, bytes_accessed=read),
        compiler_params=pltpu.CompilerParams(vmem_limit_bytes=16 << 20),
    )

    def run(*operands):
        return call(
            *(
                pltpu.with_memory_space_constraint(operand, pltpu.HBM)
                if spec is IN_PLACE
                else operand
                for operand, spec in zip(operands, in_specs, strict=True)
            )
        )

    return run


def body(
    hidden_state_input,
    attention_norm_gain,
    query_projection_matrix,
    key_projection_matrix,
    value_projection_matrix,
    output_projection_matrix,
    adapter_down_matrix,
    adapter_up_matrix,
    adapter_choice_index,
    lengths,
    rotated_key_cache,
    cached_value_rows,
):
    f32, bf16 = jnp.float32, jnp.bfloat16
    requests, width = hidden_state_input.shape
    _, cached, kv_heads, head_dim = rotated_key_cache.shape
    columns = query_projection_matrix.shape[1]
    heads = columns // head_dim
    rank = adapter_down_matrix.shape[1]
    devices = lax.axis_size("seq")
    head_size = lax.axis_size("head")
    everyone = devices * head_size
    group = heads // kv_heads
    own_rows = requests * heads // devices
    own_kv = max(own_rows // group, 1)
    parts_rows = own_rows + 2 * own_kv
    message_rows = -(-(own_rows + 2) // 8) * 8
    covering = 16 << 30
    sds = jax.ShapeDtypeStruct
    dma = pltpu.SemaphoreType.DMA

    small, scaled, up_rows, owned, table, limits = called(
        functools.partial(small_sums_kernel, own_rows),
        (
            sds((everyone, 1, requests * rank + 128), f32),
            sds((requests, width), bf16),
            sds((requests, rank, columns), bf16),
            sds((requests, 128), f32),
            sds((2, head_dim), f32),
            sds((requests, 128), jnp.int32),
        ),
        [IN_PLACE] * 6,
        [
            pltpu.SMEM((requests,), jnp.int32),
            pltpu.SMEM((requests,), jnp.int32),
            pltpu.VMEM((requests, width), bf16),
            pltpu.VMEM((width,), bf16),
            pltpu.VMEM((requests, rank, width), bf16),
            dma((4,)),
            dma((requests,)),
            dma((requests,)),
        ],
        flops=covering,
        read=covering >> 10,
    )(
        adapter_choice_index,
        lengths,
        hidden_state_input,
        attention_norm_gain,
        adapter_down_matrix,
        adapter_up_matrix,
    )
    small = lax.all_to_all(small, ("seq", "head"), 0, 0, tiled=True)
    parts = called(
        functools.partial(query_parts_kernel, width * devices),
        sds((devices, parts_rows, head_dim), bf16),
        [IN_VMEM] * 7,
        [pltpu.VMEM(((heads + 2 * kv_heads) * requests, head_dim), f32)],
        flops=covering,
        read=covering >> 10,
    )(
        owned,
        small,
        scaled,
        query_projection_matrix,
        key_projection_matrix,
        value_projection_matrix,
        up_rows,
    )
    parts = exchanged(parts)

    spread, own = called(
        functools.partial(rotation_kernel, own_kv),
        (sds((devices, own_rows, head_dim), bf16), sds((2, own_rows, head_dim), f32)),
        [IN_VMEM, IN_VMEM],
        flops=covering,
        read=covering >> 10,
    )(table, parts)
    query_rot = exchanged(spread).reshape(requests * heads, head_dim)

    entries = cached * kv_heads
    parts = called(
        functools.partial(attention_kernel, kv_heads),
        sds((devices, message_rows, head_dim), bf16),
        [IN_VMEM] * 4,
        [
            pltpu.VMEM((requests, heads, entries), bf16),
            pltpu.VMEM((requests, 2, heads, head_dim), f32),
        ],
        flops=4 * requests * heads * entries * head_dim,
        read=16 << 20,
    )(
        limits,
        query_rot,
        rotated_key_cache.reshape(requests, entries, head_dim),
        cached_value_rows.reshape(requests, entries, head_dim),
    )
    parts = exchanged(parts)
    spread = called(
        combine_kernel, sds((devices, own_rows, head_dim), bf16), [IN_VMEM, IN_VMEM]
    )(parts, own)
    attended = exchanged(spread).reshape(requests * heads, head_dim)
    out_columns = output_projection_matrix.shape[1]
    out_part = called(
        output_kernel,
        sds((requests, out_columns), f32),
        [IN_VMEM, IN_VMEM],
        [pltpu.VMEM((requests * heads, head_dim), f32)],
    )(attended, output_projection_matrix)
    if head_size == 2:
        output_sum = out_part + lax.ppermute(out_part, "head", [(0, 1), (1, 0)])
    else:
        output_sum = lax.psum(out_part, "head")
    return output_sum.astype(jnp.bfloat16)


def solution(mesh):
    return jax.shard_map(
        body,
        mesh=mesh,
        in_specs=(
            P(None, "seq"),
            P("seq"),
            P("seq", "head"),
            P("seq", "head"),
            P("seq", "head"),
            P("head", "seq"),
            P("head", None, "seq"),
            P("seq", None, "head"),
            P(),
            P(),
            P(None, "seq", "head", None),
            P(None, "seq", "head", None),
        ),
        out_specs=P(None, "seq"),
        check_vma=False,
    )
```

time: 68.1 us -> 67.7 us (level)
  blocking collectives: 43.4 us -> 57.9 us
  starting transfers between devices: 7.33 us -> 0.01 us
  waiting for transfers between devices: 5.51 us -> 1.22 us
  Pallas kernels: 10.7 us -> 7.66 us
    all_to_all x0 -> x1, blocking collectives: none -> 14.5 us  [body(): small = lax.all_to_all(small, ('seq', 'head'), 0, 0, tiled=True)]
    all_to_all x1 -> x0, starting transfers between devices: 7.33 us -> none  [body(): small = lax.all_to_all(small, ('seq', 'head'), 0, 0, tiled=True)]
    all_to_all x1 -> x0, waiting for transfers between devices: 4.29 us -> none  [body(): small = lax.all_to_all(small, ('seq', 'head'), 0, 0, tiled=True)]
    pallas_call x7 -> x6, Pallas kernels: 10.7 us -> 7.66 us  [run(): call(*(pltpu.with_memory_space_constraint(operand, pltpu.HBM) if spec is...]
  transfers between devices with their start and end apart: 2 -> 1, of which waited for: 2 -> 1; matrix products, arithmetic and copies ran while one was open for 0% -> 0% of each run, Pallas kernels for 4% -> 0%
where the time goes in v3:
time: 67.7 us; the launch traced here: 67.4 us
  blocking collectives  57.9 us (86%)
  Pallas kernels  7.66 us (11%)
  waiting for transfers between devices  1.22 us (2%)
    all_to_all x4, blocking collectives, exchanged(): return lax.all_to_all(parts, 'seq', 0, 0, tiled=True)  43.4 us
    all_to_all x1, blocking collectives, body(): small = lax.all_to_all(small, ('seq', 'head'), 0, 0, tiled=True)  14.5 us
    pallas_call x6, Pallas kernels, run(): call(*(pltpu.with_memory_space_constraint(operand, pltpu.HBM) if spec is...  7.66 us
  transfers between devices with their start and end apart: 1, of which 1 were waited for; matrix products, arithmetic and copies ran while one was open for 0% of the time, Pallas kernels for 0%

profile of v3, /device:TPU:0, one launch (start us, length us, event | category | flops | bytes accessed | tf_op | source)
XLA Modules:
  0.0 67.4 jit_solution(1330561816134660495)
XLA Ops:
  0.0 0.0 copy-start.5
  0.0 0.0 copy-start.4
  0.0 2.7 %shard_map.118 = (f32[32,1,384]{2,1,0:T(1,128)S(1)}, bf16[16,512]{1,0:T(8,128)(2,1)S(1)}, bf16[16,16,4096]{2,1,0:T(8,128)(2,1)S(1)}, f32[16,128]{1,0:T(8,128)S(1...) custom-call(s32[16]{0:T(128)} %choice_hbm.1, s32[16]{0:T(128)} %lengths_hbm.1, bf16[16,512]{1,0:T(8,128)(2,1)} %hidden_hbm.1, ...), custom_call_target="tpu_custom_call" | custom-call | flops 17179869184 | bytes 16777216 | tf_op jit(solution)/shard_map/pallas_call | solution.py:346
  2.7 14.5 %all_to_all.25.small_ref = f32[32,1,384]{2,1,0:T(1,128)S(1)} all-to-all(f32[32,1,384]{2,1,0:T(1,128)S(1)} %get-tuple-element.16), channel_id=1, replica_groups=mesh['seq'=16,'head'=2] {'seq','head'}, dimensions={0} | all-to-all | bytes 98304 | tf_op jit(solution)/shard_map/all_to_all | solution.py:421
  17.2 0.0 copy-done.5
  17.2 0.0 copy-done.4
  17.2 0.0 copy-done.3
  17.2 1.1 %shard_map.119 = bf16[16,40,128]{2,1,0:T(8,128)(2,1)S(1)} custom-call(f32[16,128]{1,0:T(8,128)S(1)} %get-tuple-element.15.owned_ref, f32[32,1,384]{2,1,0:T(1,128)S(1)} %all_to_all.25.small_ref, bf16[16,512]{1,0:T(8,128)(2,1)S(1)} %get-tuple-element.17.scaled_ref, bf16[512,4096]{1,0:T(8,128)(2,1)S(1)} %copy-done.3, bf16[512,512]{1,0:T(8,128)(2,1)S(1)} %copy-done.4, ...), custom_call_target="tpu_custom_call" | custom-call | flops 17179869184 | bytes 16777216 | tf_op jit(solution)/shard_map/pallas_call | solution.py:346
  18.3 11.0 %all_to_all.26.parts_ref = bf16[16,40,128]{2,1,0:T(8,128)(2,1)S(1)} all-to-all(bf16[16,40,128]{2,1,0:T(8,128)(2,1)S(1)} %shard_map.119), channel_id=1, replica_groups=mesh['seq'=16,'head'=2] {'seq'}, dimensions={0} | all-to-all | bytes 327680 | tf_op jit(solution)/shard_map/all_to_all | solution.py:21
  29.3 0.0 copy-start
  29.3 0.2 shard_map.120
  29.5 11.3 %all_to_all.27 = bf16[16,32,128]{2,1,0:T(8,128)(2,1)S(1)} all-to-all(bf16[16,32,128]{2,1,0:T(8,128)(2,1)S(1)} %get-tuple-element.19), channel_id=1, replica_groups=mesh['seq'=16,'head'=2] {'seq'}, dimensions={0} | all-to-all | bytes 262144 | tf_op jit(solution)/shard_map/all_to_all | solution.py:21
  40.7 0.0 copy-done
  40.7 0.0 copy-done.1
  40.7 0.0 copy-start.2
  40.7 2.6 %shard_map.121 = bf16[16,40,128]{2,1,0:T(8,128)(2,1)S(1)} custom-call(s32[16,128]{1,0:T(8,128)S(1)} %get-tuple-element.13.limits_ref, bf16[512,128]{1,0:T(8,128)(2,1)S(1)} %bitcast.6, bf16[16,1024,128]{2,1,0:T(8,128)(2,1)S(1)} %bitcast.4, bf16[16,1024,128]{2,1,0:T(8,128)(2,1)S(1)} %bitcast.5), custom_call_target="tpu_custom_call" | custom-call | flops 268435456 | bytes 16777216 | tf_op jit(solution)/shard_map/pallas_call | solution.py:346
  43.3 10.5 %all_to_all.28.parts_ref = bf16[16,40,128]{2,1,0:T(8,128)(2,1)S(1)} all-to-all(bf16[16,40,128]{2,1,0:T(8,128)(2,1)S(1)} %shard_map.121), channel_id=1, replica_groups=mesh['seq'=16,'head'=2] {'seq'}, dimensions={0} | all-to-all | bytes 327680 | tf_op jit(solution)/shard_map/all_to_all | solution.py:21
  53.9 0.4 shard_map.122
  54.3 10.6 %all_to_all.29 = bf16[16,32,128]{2,1,0:T(8,128)(2,1)S(1)} all-to-all(bf16[16,32,128]{2,1,0:T(8,128)(2,1)S(1)} %shard_map.122), channel_id=1, replica_groups=mesh['seq'=16,'head'=2] {'seq'}, dimensions={0} | all-to-all | bytes 262144 | tf_op jit(solution)/shard_map/all_to_all | solution.py:21
  65.0 0.0 copy-done.2
  65.0 0.7 shard_map.123
  65.6 0.0 collective-permute-start
  65.6 1.2 %collective-permute-done = f32[16,512]{1,0:T(8,128)S(1)} collective-permute-done((f32[16,512]{1,0:T(8,128)S(1)}, f32[16,512]{1,0:T(8,128)S(1)}, u32[]{:S(2)}, u32[]{:S(2)}) %collective-permute-start) | collective-permute-done | bytes 32800 | tf_op jit(solution)/shard_map/ppermute | solution.py:479
  66.8 0.6 add_convert_fusion
  (2 shorter events, 0.0 us)
Async XLA Ops:
  0.0 17.2 %copy-start.5 = (bf16[512,512]{1,0:T(8,128)(2,1)S(1)}, bf16[512,512]{1,0:T(8,128)(2,1)}, u32[]{:S(2)}) copy-start(bf16[512,512]{1,0:T(8,128)(2,1)} %value_ref.1) | copy-start | bytes 1572868
  0.0 17.2 %copy-start.4 = (bf16[512,512]{1,0:T(8,128)(2,1)S(1)}, bf16[512,512]{1,0:T(8,128)(2,1)}, u32[]{:S(2)}) copy-start(bf16[512,512]{1,0:T(8,128)(2,1)} %key_ref.1) | copy-start | bytes 1572868
  0.0 17.2 %copy-start.3 = (bf16[512,4096]{1,0:T(8,128)(2,1)S(1)}, bf16[512,4096]{1,0:T(8,128)(2,1)}, u32[]{:S(2)}) copy-start(bf16[512,4096]{1,0:T(8,128)(2,1)} %query_ref.1) | copy-start | bytes 12582916
  29.3 11.4 %copy-start = (bf16[16,256,4,128]{3,2,1,0:T(4,128)(2,1)S(1)}, bf16[16,256,4,128]{3,2,1,0:T(4,128)(2,1)}, u32[]{:S(2)}) copy-start(bf16[16,256,4,128]{3,2,1,0:T(4,128)(2,1)} %param.22) | copy-start | bytes 12582916
  29.3 11.4 %copy-start.1 = (bf16[16,256,4,128]{3,2,1,0:T(4,128)(2,1)S(1)}, bf16[16,256,4,128]{3,2,1,0:T(4,128)(2,1)}, u32[]{:S(2)}) copy-start(bf16[16,256,4,128]{3,2,1,0:T(4,128)(2,1)} %param.23) | copy-start | bytes 12582916
  40.7 24.2 %copy-start.2 = (bf16[4096,512]{1,0:T(8,128)(2,1)S(1)}, bf16[4096,512]{1,0:T(8,128)(2,1)}, u32[]{:S(2)}) copy-start(bf16[4096,512]{1,0:T(8,128)(2,1)} %weight_ref.1) | copy-start | bytes 12582916
  65.6 1.2 %collective-permute-start = (f32[16,512]{1,0:T(8,128)S(1)}, f32[16,512]{1,0:T(8,128)S(1)}, u32[]{:S(2)}, u32[]{:S(2)}) collective-permute-start(f32[16,512]{1,0:T(8,128)S(1)} %shard_map.123), channel_id=1, source_target_pairs={{0,1},{1,0},{2,3},{3,2},{4,5},{5,4},{6,7},{7,6},{8,9},{9,8},{10,11... | collective-permute-start | bytes 98312 | tf_op jit(solution)/shard_map/ppermute | solution.py:479

commit v4 on v3

--- a/solution.py
+++ b/solution.py
@@ -12,13 +12,17 @@
 adapter_scale_factor = 1.0
 rope_base = 500000.0
 masked_score = -1e30
+masked_limit = 5e29
 
 IN_VMEM = pl.BlockSpec(memory_space=pltpu.VMEM)
 IN_PLACE = pl.BlockSpec(memory_space=pltpu.HBM)
 
 
-def exchanged(parts):
-    return lax.all_to_all(parts, "seq", 0, 0, tiled=True)
+def exchanged(rows, axes):
+    count, head_dim = lax.axis_size(axes), rows.shape[1]
+    inner = math.gcd(rows.shape[0] // count, 8)
+    blocks = rows.reshape(count, -1, inner, head_dim)
+    return lax.all_to_all(blocks, axes, 0, 0, tiled=True).reshape(rows.shape)
 
 
 def iota(shape, axis):
@@ -47,6 +51,7 @@
 
 
 def small_sums_kernel(
+    axes,
     own_rows,
     choice_hbm,
     lengths_hbm,
@@ -109,7 +114,7 @@
     lengths_copy.wait()
     for r in range(requests):
         limits_ref[pl.ds(r, 1), :] = jnp.full((1, limits_ref.shape[1]), lengths_ref[r], jnp.int32)
-    own_request = lax.axis_index("seq") * own_rows // (columns // head_dim)
+    own_request = lax.axis_index(axes) * own_rows // (columns // head_dim)
     position = lengths_ref[own_request].astype(jnp.float32)
     half_dim = head_dim // 2
     lane = iota((1, head_dim), 1)
@@ -141,7 +146,7 @@
     keep = (iota(products.shape, 1) // rank == iota(products.shape, 0)) & owned
     sums = jnp.sum(jnp.where(keep, products, 0.0), axis=0, keepdims=True)
     message = jnp.concatenate([sums, squares], axis=1)
-    message_ref[...] = jnp.broadcast_to(message[None], message_ref.shape)
+    message_ref[...] = message
     for r in range(requests):
 
         @pl.when(up_held(r))
@@ -149,8 +154,14 @@
             up_copy(r).wait()
 
 
+def repeat_kernel(message_ref, repeated_ref):
+    repeated_ref[...] = jnp.broadcast_to(message_ref[...][None], repeated_ref.shape)
+
+
 def query_parts_kernel(
     model_width,
+    own_rows,
+    own_kv,
     owned_ref,
     small_ref,
     scaled_ref,
@@ -160,14 +171,12 @@
     up_rows_ref,
     message_ref,
     rows_ref,
+    staged_ref,
 ):
     requests, rank, columns = up_rows_ref.shape
-    devices, message_rows, head_dim = message_ref.shape
+    head_dim = message_ref.shape[1]
     heads = columns // head_dim
     kv_heads = key_ref.shape[1] // head_dim
-    all_heads = heads + 2 * kv_heads
-    own_rows = requests * heads // devices
-    own_kv = (message_rows - own_rows) // 2
     small = jnp.sum(small_ref[...], axis=0)
     sums, squares = small[:, : requests * rank], small[:, requests * rank :]
     diagonal = iota((requests, 128), 1) == iota((requests, 128), 0)
@@ -180,7 +189,10 @@
     scaled = scaled_ref[...]
     up_rows = up_rows_ref.reshape(requests * rank, columns)
     chunk = min(columns, 1024)
-    first_head = 0
+    query_places = list(range(heads))
+    key_places = [heads + k + k // own_kv * own_kv for k in range(kv_heads)]
+    value_places = [place + own_kv for place in key_places]
+    places = iter(query_places + key_places + value_places)
     for weight_ref in (query_ref, key_ref, value_ref):
         for start in range(0, weight_ref.shape[1], chunk):
             size = min(chunk, weight_ref.shape[1] - start)
@@ -193,51 +205,51 @@
                     shrunk, up_rows[:, pl.ds(start, size)], preferred_element_type=jnp.float32
                 )
             for k in range(size // head_dim):
-                h = first_head + start // head_dim + k
-                rows_ref[pl.ds(h * requests, requests), :] = part[
+                rows_ref[pl.ds(next(places) * requests, requests), :] = part[
                     :, k * head_dim : (k + 1) * head_dim
                 ]
-        first_head += weight_ref.shape[1] // head_dim
-    for t in range(devices):
+    rows = own_rows + 2 * own_kv
+    for t in range(requests * heads // own_rows):
         r, h = divmod(t * own_rows, heads)
-        kv = h * kv_heads // heads
-
-        def taken(first, count):
-            return rows_ref[pl.ds(first * requests + r, count, stride=requests), :]
-
-        if own_rows == heads:
-            block = taken(0, all_heads)
-        else:
-            block = jnp.concatenate(
-                [taken(h, own_rows), taken(heads + kv, own_kv), taken(heads + kv_heads + kv, own_kv)]
-            )
-        message_ref[t] = block.astype(jnp.bfloat16)
-
-
-def rotation_kernel(own_kv, table_ref, parts_ref, spread_ref, own_ref):
-    own_rows, head_dim = spread_ref.shape[1:]
+        kv = heads + 2 * (h * kv_heads // heads)
+        staged_ref[pl.ds(t * rows, own_rows), :] = rows_ref[
+            pl.ds(h * requests + r, own_rows, stride=requests), :
+        ]
+        staged_ref[pl.ds(t * rows + own_rows, 2 * own_kv), :] = rows_ref[
+            pl.ds(kv * requests + r, 2 * own_kv, stride=requests), :
+        ]
+    message_ref[...] = staged_ref[...].astype(jnp.bfloat16)
+
+
+def rotation_kernel(own_rows, own_kv, table_ref, parts_ref, spread_ref, own_ref):
+    head_dim = spread_ref.shape[2]
     group = own_rows // own_kv
+    rows = own_rows + 2 * own_kv
     sums = jnp.sum(parts_ref[...].astype(jnp.float32), axis=0)
     cosine, sine_val = table_ref[0:1, :], table_ref[1:2, :]
-    rotated = rounded(
-        sums * cosine + pltpu.roll(sums, head_dim // 2, 1) * sine_val
-    )
-    query_rot = rotated[:own_rows]
+    rotated = rounded(sums * cosine + pltpu.roll(sums, head_dim // 2, 1) * sine_val)
+
+    def repeated(rows, first):
+        return [
+            jnp.broadcast_to(rows[first + k : first + k + 1], (group, head_dim))
+            for k in range(own_kv)
+        ]
+
+    queries, keys, values = [], [], []
+    for first in range(0, sums.shape[0], rows):
+        queries.append(rotated[first : first + own_rows])
+        keys += repeated(rotated, first + own_rows)
+        values += repeated(rounded(sums), first + own_rows + own_kv)
+    query_rot = jnp.concatenate(queries)
     spread_ref[...] = jnp.broadcast_to(query_rot.astype(jnp.bfloat16)[None], spread_ref.shape)
-
-    def repeated(rows):
-        return jnp.concatenate(
-            [jnp.broadcast_to(rows[k : k + 1], (group, head_dim)) for k in range(own_kv)]
-        )
-
-    key_rot = repeated(rotated[own_rows : own_rows + own_kv])
-    own_score = jnp.sum(query_rot * key_rot, axis=1, keepdims=True) * head_dim ** (-0.5)
-    own_ref[0] = jnp.broadcast_to(own_score, (own_rows, head_dim))
-    own_ref[1] = repeated(rounded(sums[own_rows + own_kv : own_rows + 2 * own_kv]))
+    own_score = jnp.sum(query_rot * jnp.concatenate(keys), axis=1, keepdims=True)
+    own_ref[0] = jnp.broadcast_to(own_score * head_dim ** (-0.5), query_rot.shape)
+    own_ref[1] = jnp.concatenate(values)
 
 
 def attention_kernel(
     kv_heads,
+    own_rows,
     limits_ref,
     query_ref,
     key_ref,
@@ -245,80 +257,95 @@
     message_ref,
     weights_ref,
     stats_ref,
+    staged_ref,
 ):
     requests, entries, head_dim = key_ref.shape
     cached = entries // kv_heads
-    devices, message_rows, _ = message_ref.shape
     heads = query_ref.shape[0] // requests
-    own_rows = requests * heads // devices
     group = heads // kv_heads
     first = lax.axis_index("seq") * cached
-    shape = (heads, entries)
-    column = iota(shape, 1)
-    same_head = column % kv_heads == iota(shape, 0) // group
-    position = jnp.where(same_head, first + column // kv_heads, jnp.int32(2**30))
     lane = iota((heads, head_dim), 1)
     row = iota((heads, head_dim), 0)
+    per_tile = head_dim // kv_heads
+    position = jnp.where(
+        lane % kv_heads == row // group, first + lane // kv_heads, jnp.int32(2**30)
+    )
+    score_scale = head_dim ** (-0.5)
     for r in range(requests):
         scores = lax.dot_general(
             query_ref[pl.ds(r * heads, heads), :],
             key_ref[r],
             (((1,), (1,)), ((), ())),
             preferred_element_type=jnp.float32,
-        ) * head_dim ** (-0.5)
-        valid = position < limits_ref[pl.ds(r, 1), 0:1]
-        scores = jnp.where(valid, scores, masked_score)
-        peak = jnp.max(scores, axis=1, keepdims=True)
+        )
+        limit = jnp.broadcast_to(limits_ref[pl.ds(r, 1), :], (heads, head_dim))
+        tiles = []
+        peak = jnp.full((heads, head_dim), -masked_limit, jnp.float32)
+        for c in range(entries // head_dim):
+            valid = position < limit - c * per_tile
+            tile = scores[:, c * head_dim : (c + 1) * head_dim]
+            tiles.append(jnp.where(valid, tile, masked_score))
+            peak = jnp.maximum(peak, tiles[-1])
+        peak = jnp.max(peak, axis=1, keepdims=True)
+        total = jnp.zeros((heads, head_dim), jnp.float32)
+        for c, tile in enumerate(tiles):
+            weights = jnp.exp2((tile - peak) * (score_scale * math.log2(math.e)))
+            total = total + weights
+            weights_ref[r, :, pl.ds(c * head_dim, head_dim)] = weights.astype(jnp.bfloat16)
+        total = jnp.sum(total, axis=1, keepdims=True)
+        peak = peak * score_scale
         peak_high = rounded(peak)
         peak_mid = rounded(peak - peak_high)
         peak_low = peak - peak_high - peak_mid
-        weights = jnp.where(valid, jnp.exp(scores - peak), 0.0)
-        total = jnp.sum(weights, axis=1, keepdims=True)
         total_high = rounded(total)
         total_low = rounded(total - total_high)
-        weights_ref[r] = weights.astype(jnp.bfloat16)
         stats = jnp.zeros((heads, head_dim), jnp.float32)
-        for k, piece in enumerate((peak_high, peak_mid, peak_low, total_high)):
+        for k, piece in enumerate((peak_high, peak_mid, peak_low, total_high, total_low)):
             stats = jnp.where(lane == k * own_rows + row % own_rows, piece, stats)
-        stats_ref[r, 0] = stats
-        stats_ref[r, 1] = jnp.where(lane == row % own_rows, total_low, 0.0)
+        stats_ref[r] = stats
     for r in range(requests):
         out = jnp.dot(weights_ref[r], value_ref[r], preferred_element_type=jnp.float32)
         for part in range(heads // own_rows):
             window = slice(part * own_rows, (part + 1) * own_rows)
-            first_row = jnp.sum(stats_ref[r, 0, window, :], axis=0, keepdims=True)
-            second_row = jnp.sum(stats_ref[r, 1, window, :], axis=0, keepdims=True)
-            filler_shape = (message_rows - own_rows, head_dim)
-            filler = jnp.where(iota(filler_shape, 0) == 0, first_row, second_row)
-            block = jnp.concatenate([out[window], filler])
-            message_ref[r * (heads // own_rows) + part] = block.astype(jnp.bfloat16)
-
-
-def combine_kernel(parts_ref, own_ref, spread_ref):
-    devices, own_rows, head_dim = spread_ref.shape
+            place = (r * (heads // own_rows) + part) * (own_rows + 2)
+            stats_row = jnp.sum(stats_ref[r, window, :], axis=0, keepdims=True)
+            staged_ref[pl.ds(place, own_rows), :] = out[window]
+            staged_ref[pl.ds(place + own_rows, 2), :] = jnp.broadcast_to(stats_row, (2, head_dim))
+    message_ref[...] = staged_ref[...].astype(jnp.bfloat16)
+
+
+def combine_kernel(own_rows, parts_ref, own_ref, spread_ref, staged_ref):
+    devices, all_rows, head_dim = spread_ref.shape
+    halves = all_rows // own_rows
     lane = iota((own_rows, head_dim), 1)
     row = iota((own_rows, head_dim), 0)
-    own_score = own_ref[0][:, 0:1]
-    peaks, totals = [], []
-    overall = own_score
-    for s in range(devices):
-        stats = parts_ref[s].astype(jnp.float32)
-        first_row, second_row = stats[own_rows : own_rows + 1], stats[own_rows + 1 : own_rows + 2]
-        peak = jnp.where((lane < 3 * own_rows) & (lane % own_rows == row), first_row, 0.0)
-        total = jnp.where(lane == 3 * own_rows + row, first_row, 0.0)
-        total = total + jnp.where(lane == row, second_row, 0.0)
-        peaks.append(jnp.sum(peak, axis=1, keepdims=True))
-        totals.append(jnp.sum(total, axis=1, keepdims=True))
-        overall = jnp.maximum(overall, peaks[-1])
-    own_weight = jnp.exp(own_score - overall)
-    denominator = own_weight
-    summed = own_weight * own_ref[1]
-    for s in range(devices):
-        factor = jnp.exp(peaks[s] - overall)
-        denominator = denominator + totals[s] * factor
-        summed = summed + factor * parts_ref[s].astype(jnp.float32)[:own_rows]
-    attended = (summed / denominator).astype(jnp.bfloat16)
-    spread_ref[...] = jnp.broadcast_to(attended[None], spread_ref.shape)
+    staged_ref[...] = parts_ref[...].astype(jnp.float32)
+    same_row = lane % own_rows == row
+    for half in range(halves):
+        window = slice(half * own_rows, (half + 1) * own_rows)
+        own_score = own_ref[0, window, 0:1]
+        places = [(s * halves + half) * (own_rows + 2) for s in range(devices)]
+        peaks, totals = [], []
+        overall = own_score
+        for place in places:
+            stats = staged_ref[pl.ds(place + own_rows, 1), :]
+            stats = jnp.where(same_row & (lane < 5 * own_rows), stats, 0.0)
+            peak = jnp.where(lane < 3 * own_rows, stats, 0.0)
+            peaks.append(jnp.sum(peak, axis=1, keepdims=True))
+            total = jnp.where(lane < 3 * own_rows, 0.0, stats)
+            totals.append(jnp.sum(total, axis=1, keepdims=True))
+            overall = jnp.maximum(overall, peaks[-1])
+        own_weight = jnp.exp(own_score - overall)
+        denominator = own_weight
+        summed = own_weight * own_ref[1, window, :]
+        for place, peak, total in zip(places, peaks, totals):
+            factor = jnp.exp(peak - overall)
+            denominator = denominator + total * factor
+            summed = summed + factor * staged_ref[pl.ds(place, own_rows), :]
+        attended = (summed / denominator).astype(jnp.bfloat16)
+        spread_ref[:, window, :] = jnp.broadcast_to(
+            attended[None], (devices, own_rows, head_dim)
+        )
 
 
 def output_kernel(attended_ref, weight_ref, out_ref, rows_ref):
@@ -379,18 +406,21 @@
     head_size = lax.axis_size("head")
     everyone = devices * head_size
     group = heads // kv_heads
-    own_rows = requests * heads // devices
+    shared = requests * heads % everyone == 0
+    axes = ("seq", "head") if shared else ("seq",)
+    halves = head_size if shared else 1
+    own_rows = requests * heads // (devices * halves)
     own_kv = max(own_rows // group, 1)
     parts_rows = own_rows + 2 * own_kv
-    message_rows = -(-(own_rows + 2) // 8) * 8
+    targets = devices * halves
     covering = 16 << 30
     sds = jax.ShapeDtypeStruct
     dma = pltpu.SemaphoreType.DMA
 
     small, scaled, up_rows, owned, table, limits = called(
-        functools.partial(small_sums_kernel, own_rows),
+        functools.partial(small_sums_kernel, axes, own_rows),
         (
-            sds((everyone, 1, requests * rank + 128), f32),
+            sds((1, requests * rank + 128), f32),
             sds((requests, width), bf16),
             sds((requests, rank, columns), bf16),
             sds((requests, 128), f32),
@@ -408,8 +438,6 @@
             dma((requests,)),
             dma((requests,)),
         ],
-        flops=covering,
-        read=covering >> 10,
     )(
         adapter_choice_index,
         lengths,
@@ -418,12 +446,22 @@
         adapter_down_matrix,
         adapter_up_matrix,
     )
+    small = called(
+        repeat_kernel,
+        sds((everyone,) + small.shape, f32),
+        [IN_VMEM],
+        flops=covering,
+        read=covering >> 10,
+    )(small)
     small = lax.all_to_all(small, ("seq", "head"), 0, 0, tiled=True)
     parts = called(
-        functools.partial(query_parts_kernel, width * devices),
-        sds((devices, parts_rows, head_dim), bf16),
+        functools.partial(query_parts_kernel, width * devices, own_rows, own_kv),
+        sds((targets * parts_rows, head_dim), bf16),
         [IN_VMEM] * 7,
-        [pltpu.VMEM(((heads + 2 * kv_heads) * requests, head_dim), f32)],
+        [
+            pltpu.VMEM(((heads + 2 * kv_heads) * requests, head_dim), f32),
+            pltpu.VMEM((targets * parts_rows, head_dim), f32),
+        ],
         flops=covering,
         read=covering >> 10,
     )(
@@ -435,25 +473,28 @@
         value_projection_matrix,
         up_rows,
     )
-    parts = exchanged(parts)
-
+    parts = exchanged(parts, axes).reshape(devices, halves * parts_rows, head_dim)
     spread, own = called(
-        functools.partial(rotation_kernel, own_kv),
-        (sds((devices, own_rows, head_dim), bf16), sds((2, own_rows, head_dim), f32)),
+        functools.partial(rotation_kernel, own_rows, own_kv),
+        (
+            sds((devices, halves * own_rows, head_dim), bf16),
+            sds((2, halves * own_rows, head_dim), f32),
+        ),
         [IN_VMEM, IN_VMEM],
         flops=covering,
         read=covering >> 10,
     )(table, parts)
-    query_rot = exchanged(spread).reshape(requests * heads, head_dim)
+    query_rot = exchanged(spread.reshape(-1, head_dim), axes)
 
     entries = cached * kv_heads
     parts = called(
-        functools.partial(attention_kernel, kv_heads),
-        sds((devices, message_rows, head_dim), bf16),
+        functools.partial(attention_kernel, kv_heads, own_rows),
+        sds((targets * (own_rows + 2), head_dim), bf16),
         [IN_VMEM] * 4,
         [
             pltpu.VMEM((requests, heads, entries), bf16),
-            pltpu.VMEM((requests, 2, heads, head_dim), f32),
+            pltpu.VMEM((requests, heads, head_dim), f32),
+            pltpu.VMEM((targets * (own_rows + 2), head_dim), f32),
         ],
         flops=4 * requests * heads * entries * head_dim,
         read=16 << 20,
@@ -463,11 +504,14 @@
         rotated_key_cache.reshape(requests, entries, head_dim),
         cached_value_rows.reshape(requests, entries, head_dim),
     )
-    parts = exchanged(parts)
+    parts = exchanged(parts, axes)
     spread = called(
-        combine_kernel, sds((devices, own_rows, head_dim), bf16), [IN_VMEM, IN_VMEM]
+        functools.partial(combine_kernel, own_rows),
+        sds((devices, halves * own_rows, head_dim), bf16),
+        [IN_VMEM, IN_VMEM],
+        [pltpu.VMEM(parts.shape, f32)],
     )(parts, own)
-    attended = exchanged(spread).reshape(requests * heads, head_dim)
+    attended = exchanged(spread.reshape(-1, head_dim), axes)
     out_columns = output_projection_matrix.shape[1]
     out_part = called(
         output_kernel,

time: 67.7 us -> 64.4 us (0.951)
  blocking collectives: 57.9 us -> 55.2 us
  Pallas kernels: 7.66 us -> 6.86 us
    all_to_all x4, blocking collectives: 43.4 us -> 40.8 us  [exchanged(): return lax.all_to_all(blocks, axes, 0, 0, tiled=True).reshape(rows.shape)]
    pallas_call x6 -> x7, Pallas kernels: 7.66 us -> 6.86 us  [run(): call(*(pltpu.with_memory_space_constraint(operand, pltpu.HBM) if spec is...]
where the time goes in v4:
time: 64.4 us; the launch traced here: 64 us
  blocking collectives  55.2 us (86%)
  Pallas kernels  6.86 us (11%)
  waiting for transfers between devices  0.99 us (2%)
    all_to_all x4, blocking collectives, exchanged(): return lax.all_to_all(blocks, axes, 0, 0, tiled=True).reshape(rows.shape)  40.8 us
    all_to_all x1, blocking collectives, body(): small = lax.all_to_all(small, ('seq', 'head'), 0, 0, tiled=True)  14.5 us
    pallas_call x7, Pallas kernels, run(): call(*(pltpu.with_memory_space_constraint(operand, pltpu.HBM) if spec is...  6.86 us
  transfers between devices with their start and end apart: 1, of which 1 were waited for; matrix products, arithmetic and copies ran while one was open for 0% of the time, Pallas kernels for 0%

profile of v4, /device:TPU:0, one launch (start us, length us, event | category | flops | bytes accessed | tf_op | source)
XLA Modules:
  0.0 64.0 jit_solution(4815986157201314518)
XLA Ops:
  0.0 2.2 %shard_map.118 = (f32[1,384]{1,0:T(1,128)S(1)}, bf16[16,512]{1,0:T(8,128)(2,1)S(1)}, bf16[16,16,4096]{2,1,0:T(8,128)(2,1)S(1)}, f32[16,128]{1,0:T(8,128)S(1)}, f...) custom-call(s32[16]{0:T(128)} %choice_hbm.1, s32[16]{0:T(128)} %lengths_hbm.1, bf16[16,512]{1,0:T(8,128)(2,1)} %hidden_hbm.1, ...), custom_call_target="tpu_custom_call" | custom-call | tf_op jit(solution)/shard_map/pallas_call | solution.py:373
  2.2 0.0 copy-start.3
  2.2 0.0 copy-start.4
  2.2 0.0 copy-start.5
  2.3 14.5 %all_to_all.25.small_ref = f32[32,1,384]{2,1,0:T(1,128)S(1)} all-to-all(f32[32,1,384]{2,1,0:T(1,128)S(1)} %shard_map.119), channel_id=1, replica_groups=mesh['seq'=16,'head'=2] {'seq','head'}, dimensions={0} | all-to-all | bytes 98304 | tf_op jit(solution)/shard_map/all_to_all | solution.py:456
  16.7 0.0 copy-done.3
  16.7 0.0 copy-done.4
  16.7 0.0 copy-done.5
  16.7 1.1 %shard_map.120 = bf16[640,128]{1,0:T(8,128)(2,1)S(1)} custom-call(f32[16,128]{1,0:T(8,128)S(1)} %get-tuple-element.15.owned_ref, f32[32,1,384]{2,1,0:T(1,128)S(1)} %all_to_all.25.small_ref, bf16[16,512]{1,0:T(8,128)(2,1)S(1)} %get-tuple-element.17.scaled_ref, bf16[512,4096]{1,0:T(8,128)(2,1)S(1)} %copy-done.3, bf16[512,512]{1,0:T(8,128)(2,1)S(1)} %copy-done.4, ...), custom_call_target="tpu_custom_call" | custom-call | flops 17179869184 | bytes 16777216 | tf_op jit(solution)/shard_map/pallas_call | solution.py:373
  17.9 10.3 %all_to_all.26 = bf16[32,5,4,128]{3,2,1,0:T(4,128)(2,1)S(1)} all-to-all(bf16[32,5,4,128]{3,2,1,0:T(4,128)(2,1)S(1)} %bitcast.17), channel_id=1, replica_groups=mesh['seq'=16,'head'=2] {'seq','head'}, dimensions={0} | all-to-all | bytes 327680 | tf_op jit(solution)/shard_map/all_to_all | solution.py:25
  28.2 0.0 copy-start
  28.2 0.2 shard_map.121
  28.4 10.2 %all_to_all.27 = bf16[32,2,8,128]{3,2,1,0:T(8,128)(2,1)S(1)} all-to-all(bf16[32,2,8,128]{3,2,1,0:T(8,128)(2,1)S(1)} %bitcast.19), channel_id=1, replica_groups=mesh['seq'=16,'head'=2] {'seq','head'}, dimensions={0} | all-to-all | bytes 262144 | tf_op jit(solution)/shard_map/all_to_all | solution.py:25
  38.6 0.0 copy-done
  38.6 0.0 copy-done.1
  38.6 2.3 %shard_map.122 = bf16[576,128]{1,0:T(8,128)(2,1)S(1)} custom-call(s32[16,128]{1,0:T(8,128)S(1)} %get-tuple-element.13.limits_ref, bf16[512,128]{1,0:T(8,128)(2,1)S(1)} %bitcast.14, bf16[16,1024,128]{2,1,0:T(8,128)(2,1)S(1)} %bitcast.10, bf16[16,1024,128]{2,1,0:T(8,128)(2,1)S(1)} %bitcast.11), custom_call_target="tpu_custom_call" | custom-call | flops 268435456 | bytes 16777216 | tf_op jit(solution)/shard_map/pallas_call | solution.py:373
  40.9 10.2 %all_to_all.28 = bf16[32,9,2,128]{3,2,1,0:T(2,128)(2,1)S(1)} all-to-all(bf16[32,9,2,128]{3,2,1,0:T(2,128)(2,1)S(1)} %bitcast.13), channel_id=1, replica_groups=mesh['seq'=16,'head'=2] {'seq','head'}, dimensions={0} | all-to-all | bytes 294912 | tf_op jit(solution)/shard_map/all_to_all | solution.py:25
  51.1 0.4 shard_map.123
  51.4 10.1 %all_to_all.29 = bf16[32,2,8,128]{3,2,1,0:T(8,128)(2,1)S(1)} all-to-all(bf16[32,2,8,128]{3,2,1,0:T(8,128)(2,1)S(1)} %bitcast.16), channel_id=1, replica_groups=mesh['seq'=16,'head'=2] {'seq','head'}, dimensions={0} | all-to-all | bytes 262144 | tf_op jit(solution)/shard_map/all_to_all | solution.py:25
  61.5 0.0 copy-done.2
  61.5 0.7 %shard_map.124 = f32[16,512]{1,0:T(8,128)S(1)} custom-call(bf16[512,128]{1,0:T(8,128)(2,1)S(1)} %bitcast.15, bf16[4096,512]{1,0:T(8,128)(2,1)S(1)} %copy-done.2), custom_call_target="tpu_custom_call" | custom-call | tf_op jit(solution)/shard_map/pallas_call | solution.py:373
  62.2 0.2 collective-permute-start
  62.4 1.0 %collective-permute-done = f32[16,512]{1,0:T(8,128)S(1)} collective-permute-done((f32[16,512]{1,0:T(8,128)S(1)}, f32[16,512]{1,0:T(8,128)S(1)}, u32[]{:S(2)}, u32[]{:S(2)}) %collective-permute-start) | collective-permute-done | bytes 32800 | tf_op jit(solution)/shard_map/ppermute | solution.py:523
  63.4 0.6 add_convert_fusion
  (3 shorter events, 0.0 us)
Async XLA Ops:
  2.2 14.5 %copy-start.3 = (bf16[512,4096]{1,0:T(8,128)(2,1)S(1)}, bf16[512,4096]{1,0:T(8,128)(2,1)}, u32[]{:S(2)}) copy-start(bf16[512,4096]{1,0:T(8,128)(2,1)} %query_ref.1) | copy-start | bytes 12582916
  2.2 14.5 %copy-start.4 = (bf16[512,512]{1,0:T(8,128)(2,1)S(1)}, bf16[512,512]{1,0:T(8,128)(2,1)}, u32[]{:S(2)}) copy-start(bf16[512,512]{1,0:T(8,128)(2,1)} %key_ref.1) | copy-start | bytes 1572868
  2.2 14.5 %copy-start.5 = (bf16[512,512]{1,0:T(8,128)(2,1)S(1)}, bf16[512,512]{1,0:T(8,128)(2,1)}, u32[]{:S(2)}) copy-start(bf16[512,512]{1,0:T(8,128)(2,1)} %value_ref.1) | copy-start | bytes 1572868
  28.2 10.3 %copy-start = (bf16[16,256,4,128]{3,2,1,0:T(4,128)(2,1)S(1)}, bf16[16,256,4,128]{3,2,1,0:T(4,128)(2,1)}, u32[]{:S(2)}) copy-start(bf16[16,256,4,128]{3,2,1,0:T(4,128)(2,1)} %param.22) | copy-start | bytes 12582916
  28.2 10.3 %copy-start.1 = (bf16[16,256,4,128]{3,2,1,0:T(4,128)(2,1)S(1)}, bf16[16,256,4,128]{3,2,1,0:T(4,128)(2,1)}, u32[]{:S(2)}) copy-start(bf16[16,256,4,128]{3,2,1,0:T(4,128)(2,1)} %param.23) | copy-start | bytes 12582916
  38.6 23.0 %copy-start.2 = (bf16[4096,512]{1,0:T(8,128)(2,1)S(1)}, bf16[4096,512]{1,0:T(8,128)(2,1)}, u32[]{:S(2)}) copy-start(bf16[4096,512]{1,0:T(8,128)(2,1)} %weight_ref.1) | copy-start | bytes 12582916
  62.2 1.2 %collective-permute-start = (f32[16,512]{1,0:T(8,128)S(1)}, f32[16,512]{1,0:T(8,128)S(1)}, u32[]{:S(2)}, u32[]{:S(2)}) collective-permute-start(f32[16,512]{1,0:T(8,128)S(1)} %shard_map.124), channel_id=1, source_target_pairs={{0,1},{1,0},{2,3},{3,2},{4,5},{5,4},{6,7},{7,6},{8,9},{9,8},{10,11... | collective-permute-start | bytes 98312 | tf_op jit(solution)/shard_map/ppermute | solution.py:523

commit v5 on v4

--- a/solution.py
+++ b/solution.py
@@ -255,6 +255,7 @@
     key_ref,
     value_ref,
     message_ref,
+    scores_ref,
     weights_ref,
     stats_ref,
     staged_ref,
@@ -272,18 +273,19 @@
     )
     score_scale = head_dim ** (-0.5)
     for r in range(requests):
-        scores = lax.dot_general(
+        scores_ref[r] = lax.dot_general(
             query_ref[pl.ds(r * heads, heads), :],
             key_ref[r],
             (((1,), (1,)), ((), ())),
             preferred_element_type=jnp.float32,
         )
-        limit = jnp.broadcast_to(limits_ref[pl.ds(r, 1), :], (heads, head_dim))
+    for r in range(requests):
+        limit = limits_ref[pl.ds(r, 1), :]
         tiles = []
         peak = jnp.full((heads, head_dim), -masked_limit, jnp.float32)
         for c in range(entries // head_dim):
             valid = position < limit - c * per_tile
-            tile = scores[:, c * head_dim : (c + 1) * head_dim]
+            tile = scores_ref[r, :, pl.ds(c * head_dim, head_dim)]
             tiles.append(jnp.where(valid, tile, masked_score))
             peak = jnp.maximum(peak, tiles[-1])
         peak = jnp.max(peak, axis=1, keepdims=True)
@@ -492,6 +494,7 @@
         sds((targets * (own_rows + 2), head_dim), bf16),
         [IN_VMEM] * 4,
         [
+            pltpu.VMEM((requests, heads, entries), f32),
             pltpu.VMEM((requests, heads, entries), bf16),
             pltpu.VMEM((requests, heads, head_dim), f32),
             pltpu.VMEM((targets * (own_rows + 2), head_dim), f32),

time: 64.4 us -> 64.5 us (level)
  no operation moved by 1% of the time
where the time goes in v5:
time: 64.5 us; the launch traced here: 64.1 us
  blocking collectives  55.2 us (86%)
  Pallas kernels  6.98 us (11%)
  waiting for transfers between devices  0.99 us (2%)
    all_to_all x4, blocking collectives, exchanged(): return lax.all_to_all(blocks, axes, 0, 0, tiled=True).reshape(rows.shape)  40.8 us
    all_to_all x1, blocking collectives, body(): small = lax.all_to_all(small, ('seq', 'head'), 0, 0, tiled=True)  14.5 us
    pallas_call x7, Pallas kernels, run(): call(*(pltpu.with_memory_space_constraint(operand, pltpu.HBM) if spec is...  6.98 us
  transfers between devices with their start and end apart: 1, of which 1 were waited for; matrix products, arithmetic and copies ran while one was open for 0% of the time, Pallas kernels for 0%

profile of v5, /device:TPU:0, one launch (start us, length us, event | category | flops | bytes accessed | tf_op | source)
XLA Modules:
  0.0 64.1 jit_solution(2376564609663693973)
XLA Ops:
  0.0 2.3 %shard_map.118 = (f32[1,384]{1,0:T(1,128)S(1)}, bf16[16,512]{1,0:T(8,128)(2,1)S(1)}, bf16[16,16,4096]{2,1,0:T(8,128)(2,1)S(1)}, f32[16,128]{1,0:T(8,128)S(1)}, f...) custom-call(s32[16]{0:T(128)} %choice_hbm.1, s32[16]{0:T(128)} %lengths_hbm.1, bf16[16,512]{1,0:T(8,128)(2,1)} %hidden_hbm.1, ...), custom_call_target="tpu_custom_call" | custom-call | tf_op jit(solution)/shard_map/pallas_call | solution.py:375
  2.3 0.0 copy-start.3
  2.3 0.0 copy-start.4
  2.3 0.0 copy-start.5
  2.4 14.5 %all_to_all.25.small_ref = f32[32,1,384]{2,1,0:T(1,128)S(1)} all-to-all(f32[32,1,384]{2,1,0:T(1,128)S(1)} %shard_map.119), channel_id=1, replica_groups=mesh['seq'=16,'head'=2] {'seq','head'}, dimensions={0} | all-to-all | bytes 98304 | tf_op jit(solution)/shard_map/all_to_all | solution.py:458
  16.8 0.0 copy-done.3
  16.8 0.0 copy-done.4
  16.8 0.0 copy-done.5
  16.8 1.1 %shard_map.120 = bf16[640,128]{1,0:T(8,128)(2,1)S(1)} custom-call(f32[16,128]{1,0:T(8,128)S(1)} %get-tuple-element.15.owned_ref, f32[32,1,384]{2,1,0:T(1,128)S(1)} %all_to_all.25.small_ref, bf16[16,512]{1,0:T(8,128)(2,1)S(1)} %get-tuple-element.17.scaled_ref, bf16[512,4096]{1,0:T(8,128)(2,1)S(1)} %copy-done.3, bf16[512,512]{1,0:T(8,128)(2,1)S(1)} %copy-done.4, ...), custom_call_target="tpu_custom_call" | custom-call | flops 17179869184 | bytes 16777216 | tf_op jit(solution)/shard_map/pallas_call | solution.py:375
  18.0 10.3 %all_to_all.26 = bf16[32,5,4,128]{3,2,1,0:T(4,128)(2,1)S(1)} all-to-all(bf16[32,5,4,128]{3,2,1,0:T(4,128)(2,1)S(1)} %bitcast.17), channel_id=1, replica_groups=mesh['seq'=16,'head'=2] {'seq','head'}, dimensions={0} | all-to-all | bytes 327680 | tf_op jit(solution)/shard_map/all_to_all | solution.py:25
  28.3 0.0 copy-start
  28.3 0.2 shard_map.121
  28.5 10.2 %all_to_all.27 = bf16[32,2,8,128]{3,2,1,0:T(8,128)(2,1)S(1)} all-to-all(bf16[32,2,8,128]{3,2,1,0:T(8,128)(2,1)S(1)} %bitcast.19), channel_id=1, replica_groups=mesh['seq'=16,'head'=2] {'seq','head'}, dimensions={0} | all-to-all | bytes 262144 | tf_op jit(solution)/shard_map/all_to_all | solution.py:25
  38.7 0.0 copy-done
  38.7 0.0 copy-done.1
  38.7 2.4 %shard_map.122 = bf16[576,128]{1,0:T(8,128)(2,1)S(1)} custom-call(s32[16,128]{1,0:T(8,128)S(1)} %get-tuple-element.13.limits_ref, bf16[512,128]{1,0:T(8,128)(2,1)S(1)} %bitcast.14, bf16[16,1024,128]{2,1,0:T(8,128)(2,1)S(1)} %bitcast.10, bf16[16,1024,128]{2,1,0:T(8,128)(2,1)S(1)} %bitcast.11), custom_call_target="tpu_custom_call" | custom-call | flops 268435456 | bytes 16777216 | tf_op jit(solution)/shard_map/pallas_call | solution.py:375
  41.0 10.2 %all_to_all.28 = bf16[32,9,2,128]{3,2,1,0:T(2,128)(2,1)S(1)} all-to-all(bf16[32,9,2,128]{3,2,1,0:T(2,128)(2,1)S(1)} %bitcast.13), channel_id=1, replica_groups=mesh['seq'=16,'head'=2] {'seq','head'}, dimensions={0} | all-to-all | bytes 294912 | tf_op jit(solution)/shard_map/all_to_all | solution.py:25
  51.2 0.4 shard_map.123
  51.5 10.1 %all_to_all.29 = bf16[32,2,8,128]{3,2,1,0:T(8,128)(2,1)S(1)} all-to-all(bf16[32,2,8,128]{3,2,1,0:T(8,128)(2,1)S(1)} %bitcast.16), channel_id=1, replica_groups=mesh['seq'=16,'head'=2] {'seq','head'}, dimensions={0} | all-to-all | bytes 262144 | tf_op jit(solution)/shard_map/all_to_all | solution.py:25
  61.7 0.0 copy-done.2
  61.7 0.7 %shard_map.124 = f32[16,512]{1,0:T(8,128)S(1)} custom-call(bf16[512,128]{1,0:T(8,128)(2,1)S(1)} %bitcast.15, bf16[4096,512]{1,0:T(8,128)(2,1)S(1)} %copy-done.2), custom_call_target="tpu_custom_call" | custom-call | tf_op jit(solution)/shard_map/pallas_call | solution.py:375
  62.3 0.2 collective-permute-start
  62.5 1.0 %collective-permute-done = f32[16,512]{1,0:T(8,128)S(1)} collective-permute-done((f32[16,512]{1,0:T(8,128)S(1)}, f32[16,512]{1,0:T(8,128)S(1)}, u32[]{:S(2)}, u32[]{:S(2)}) %collective-permute-start) | collective-permute-done | bytes 32800 | tf_op jit(solution)/shard_map/ppermute | solution.py:526
  63.5 0.6 add_convert_fusion
  (3 shorter events, 0.0 us)
Async XLA Ops:
  2.3 14.5 %copy-start.3 = (bf16[512,4096]{1,0:T(8,128)(2,1)S(1)}, bf16[512,4096]{1,0:T(8,128)(2,1)}, u32[]{:S(2)}) copy-start(bf16[512,4096]{1,0:T(8,128)(2,1)} %query_ref.1) | copy-start | bytes 12582916
  2.3 14.5 %copy-start.4 = (bf16[512,512]{1,0:T(8,128)(2,1)S(1)}, bf16[512,512]{1,0:T(8,128)(2,1)}, u32[]{:S(2)}) copy-start(bf16[512,512]{1,0:T(8,128)(2,1)} %key_ref.1) | copy-start | bytes 1572868
  2.3 14.5 %copy-start.5 = (bf16[512,512]{1,0:T(8,128)(2,1)S(1)}, bf16[512,512]{1,0:T(8,128)(2,1)}, u32[]{:S(2)}) copy-start(bf16[512,512]{1,0:T(8,128)(2,1)} %value_ref.1) | copy-start | bytes 1572868
  28.3 10.3 %copy-start = (bf16[16,256,4,128]{3,2,1,0:T(4,128)(2,1)S(1)}, bf16[16,256,4,128]{3,2,1,0:T(4,128)(2,1)}, u32[]{:S(2)}) copy-start(bf16[16,256,4,128]{3,2,1,0:T(4,128)(2,1)} %param.22) | copy-start | bytes 12582916
  28.3 10.3 %copy-start.1 = (bf16[16,256,4,128]{3,2,1,0:T(4,128)(2,1)S(1)}, bf16[16,256,4,128]{3,2,1,0:T(4,128)(2,1)}, u32[]{:S(2)}) copy-start(bf16[16,256,4,128]{3,2,1,0:T(4,128)(2,1)} %param.23) | copy-start | bytes 12582916
  38.7 23.0 %copy-start.2 = (bf16[4096,512]{1,0:T(8,128)(2,1)S(1)}, bf16[4096,512]{1,0:T(8,128)(2,1)}, u32[]{:S(2)}) copy-start(bf16[4096,512]{1,0:T(8,128)(2,1)} %weight_ref.1) | copy-start | bytes 12582916
  62.3 1.2 %collective-permute-start = (f32[16,512]{1,0:T(8,128)S(1)}, f32[16,512]{1,0:T(8,128)S(1)}, u32[]{:S(2)}, u32[]{:S(2)}) collective-permute-start(f32[16,512]{1,0:T(8,128)S(1)} %shard_map.124), channel_id=1, source_target_pairs={{0,1},{1,0},{2,3},{3,2},{4,5},{5,4},{6,7},{7,6},{8,9},{9,8},{10,11... | collective-permute-start | bytes 98312 | tf_op jit(solution)/shard_map/ppermute | solution.py:526
